TPU v7x, 32 devices: a whole 2x2x4 slice. The times are simulated.
32 devices in a mesh: rep: 4 (over y, x), shard: 8 (over z, core).
Axes of the slice: x: 2, y: 2, z: 4, core: 2. Of those that a mesh axis runs over, the one named last changes fastest.
Arguments:
- tokens: bfloat16 [16384, 768], P(('rep', 'shard')), may hold values from -6 to 6
- joined_weight: bfloat16 [768, 2304], P('shard'), may hold values from -0.21875 to 0.21875
- mixing_weight: bfloat16 [768, 768], P('shard'), may hold values from -1.25 to 1.25
- gate_weight: bfloat16 [768, 3072], P('shard'), may hold values from -0.21875 to 0.21875
- up_weight: bfloat16 [768, 3072], P('shard'), may hold values from -0.21875 to 0.21875
- down_weight: bfloat16 [3072, 768], P('shard'), may hold values from -0.15625 to 0.15625
- inner_gain: bfloat16 [768], P('shard'), may hold values from 0.5 to 1.5
- inner_shift: bfloat16 [768], P('shard'), may hold values from -1.5 to 1.5
- outer_gain: bfloat16 [768], P('shard'), may hold values from 0.5 to 1.5
- outer_shift: bfloat16 [768], P('shard'), may hold values from -1.5 to 1.5
- segments: int32 [32, 512], P(('rep', 'shard')), may hold values from 0 to 3, as said below
- positions: int32 [32, 512], P(('rep', 'shard')), may hold values from 0 to 255, as said below
- cotangent: bfloat16 [16384, 768], P(('rep', 'shard')), may hold values from -6 to 6
Outputs:
- layer_output: bfloat16 [16384, 768], P(('rep', 'shard'))
- input_grad: bfloat16 [16384, 768], P(('rep', 'shard'))
- joined_grad: float32 [768, 2304], P('shard')
- mixing_grad: float32 [768, 768], P('shard')
- gate_grad: float32 [768, 3072], P('shard')
- up_grad: float32 [768, 3072], P('shard')
- down_grad: float32 [3072, 768], P('shard')
- innergain_grad: float32 [768], P('shard')
- innershift_grad: float32 [768], P('shard')
- outergain_grad: float32 [768], P('shard')
- outershift_grad: float32 [768], P('shard')
Inputs may be any that keep to these rules, and one draw needn't show every extreme that they name: `segments`: each sequence of 512 tokens packs 4 documents in order: segment numbers never fall along a sequence and each appears; each document holds 32 to 256 tokens, and exactly one holds 256. `positions`: A token's position counts the tokens before it in its own document.
All inputs are finite; a program needn't handle non-finite values.
Results may differ from a plain program's by a relative error of at most 0.02.
Values may be sent and summed in bfloat16 or wider, within the bound.
A program may use at most 128 MiB of HBM per device.

v0:
```python
import functools
import math

import jax
import jax.numpy as jnp
import numpy as np
from jax import lax
from jax.experimental import pallas as pl
from jax.experimental.pallas import tpu as pltpu
from jax.sharding import PartitionSpec as P

H = 12
HD = 64

EPSILON = 1e-12
NEG_LARGE = -1e30
LANES = 128
MESH = pl.DeviceIdType.MESH
VMEM_LIMIT = 62 * 1024 * 1024
SLACK = 2
AHEAD = 3


class Plan:
    def __init__(self, width, replicas, shards):
        self.replicas, self.shards = replicas, shards
        self.chips = shards // 2
        self.levels = replicas.bit_length() - 1
        self.orders = 2 if self.levels > 1 and width % (2 * replicas * LANES) == 0 else 1
        self.ways = (tuple(range(self.levels)), tuple(reversed(range(self.levels))))[: self.orders]
        self.piece = width // (replicas * self.orders)
        self.width = width

    def flip(self, rep, bit):
        return rep + (1 << bit) * (1 - 2 * lax.rem(lax.div(rep, 1 << bit), 2))

    def with_bits(self, rep, bits, number):
        for at, bit in enumerate(bits):
            had = lax.rem(lax.div(rep, 1 << bit), 2)
            rep = rep + (1 << bit) * (((number >> at) & 1) - had)
        return rep

    def column(self, rep, order):
        return pl.multiple_of((rep * self.orders + order) * self.piece, LANES)

    def grow(self, rep, order, step):
        bits = self.ways[order][:step]
        return [self.with_bits(rep, bits, number) for number in range(1 << step)]

    def grow_at(self, step):
        return (1 << step) - 1

    def halve(self, rep, order, step):
        bits = self.ways[order][step + 1 :]
        return [self.with_bits(rep, bits, number) for number in range(1 << len(bits))]

    def halve_at(self, step):
        return sum(1 << (self.levels - 1 - at) for at in range(step))


def peer(rep, shard):
    return {"rep": rep, "shard": shard}


def remote(src, dst, send, recv, rep, shard):
    return pltpu.make_async_remote_copy(
        src_ref=src,
        dst_ref=dst,
        send_sem=send,
        recv_sem=recv,
        device_id=peer(rep, shard),
        device_id_type=MESH,
    )


def greet_all(plan, rep, shard):
    barrier = pltpu.get_barrier_semaphore()
    total = plan.replicas * plan.shards

    def hello(step, carry):
        other = lax.rem(rep * plan.shards + shard + step, total)
        pl.semaphore_signal(
            barrier,
            inc=1,
            device_id=peer(lax.div(other, plan.shards), lax.rem(other, plan.shards)),
            device_id_type=MESH,
        )
        return carry

    lax.fori_loop(1, total, hello, 0)
    pl.semaphore_wait(barrier, total - 1)


def greet_near(plan, rep, shard):
    barrier = pltpu.get_barrier_semaphore()
    for step in range(1, plan.shards):
        pl.semaphore_signal(
            barrier,
            inc=1,
            device_id=peer(rep, lax.rem(shard + step, plan.shards)),
            device_id_type=MESH,
        )
    for bit in range(plan.levels):
        pl.semaphore_signal(
            barrier, inc=1, device_id=peer(plan.flip(rep, bit), shard), device_id_type=MESH
        )
    pl.semaphore_wait(barrier, plan.shards - 1 + plan.levels)


def product(left, right, left_axis, right_axis):
    return lax.dot_general(
        left, right, (((left_axis,), (right_axis,)), ((), ())), preferred_element_type=jnp.float32
    )


def forward_pair(pair, query, key, value, mask_bias, attended, logsum):
    length = query.shape[0]
    block = min(length, 256)
    span = pl.ds(pl.multiple_of(pair * LANES, LANES), LANES)
    lane = lax.broadcasted_iota(jnp.int32, (1, LANES), 1)
    keys, values = key[:, span], value[:, span]
    parts = [0.0] * (length // block)
    for half in range(LANES // HD):
        pick = jnp.where(lane // HD == half, 1.0, 0.0).astype(jnp.bfloat16)
        scaled = pick * jnp.bfloat16(1.0 / math.sqrt(HD))
        picked = values * pick
        for at in range(length // block):
            rows = slice(at * block, (at + 1) * block)
            scores = product(keys, query[rows, span] * scaled, 1, 1) + mask_bias[:, rows]
            highest = jnp.max(scores, axis=0, keepdims=True)
            shifted = jnp.exp(scores - highest)
            denominator = jnp.sum(shifted, axis=0, keepdims=True)
            logsum[pl.ds(pair * (LANES // HD) + half, 1), rows] = highest + jnp.log(denominator)
            probs = (shifted * (1.0 / denominator)).astype(jnp.bfloat16)
            parts[at] += product(probs, picked, 0, 0)
    for at, part in enumerate(parts):
        attended[at * block : (at + 1) * block, span] = part.astype(jnp.bfloat16)


def gather_kernel(plan, *refs):
    own, small = refs[:4], refs[4]
    carried = refs[5:9]
    full, small_all = refs[9:13], refs[13]
    results = refs[14:23]
    stages = refs[23:27]
    (load_sem, store_sem, small_send, small_recv, z_send, z_recv, rep_send, rep_recv, core_send,
     core_recv) = refs[27:37]
    tokens, marks, segment_across, rates = refs[37:41]
    near = refs[41:50]
    query, key, value, attended, logsum, inner_resid, cosine, before, after = near
    weight, mask_bias, fetch_sem, weight_sem, result_sem = refs[50:55]
    rep, shard = lax.axis_index("rep"), lax.axis_index("shard")
    chips, piece = plan.chips, plan.piece
    place, core = lax.div(shard, 2), lax.rem(shard, 2)
    mate = place * 2 + (1 - core)
    rows = own[0].shape[0]
    length, width = tokens.shape
    pairs = width // LANES

    def part(ref, mat, top, section_rep, order):
        if mat < 3:
            return ref.at[
                pl.ds(pl.multiple_of(top, 8), rows),
                pl.ds(plan.column(section_rep, order), piece),
            ]
        per = own[3].shape[1] // piece
        section = section_rep * plan.orders + order
        return ref.at[
            pl.ds(pl.multiple_of(top + lax.div(section, per) * rows, 8), rows),
            pl.ds(pl.multiple_of(lax.rem(section, per) * piece, LANES), piece),
        ]

    def slab_part(mat, slab, section_rep, order):
        return part(full[mat], mat, slab * own[mat].shape[0], section_rep, order)

    def slab_of(mat, slab):
        deep = own[mat].shape[0]
        return full[mat].at[pl.ds(pl.multiple_of(slab * deep, 8), deep), :]

    sent = []

    def launch(copy):
        copy.start()
        sent.append(copy)

    loads = [pltpu.make_async_copy(own[mat], stages[mat], load_sem.at[mat]) for mat in range(4)]
    for load in loads:
        load.start()
    fetches = [
        pltpu.make_async_copy(far, here, fetch_sem.at[at])
        for at, (far, here) in enumerate(zip(carried, (tokens, marks, segment_across, rates)))
    ]
    for fetch in fetches:
        fetch.start()
    small_all[shard] = small[...]
    greet_near(plan, rep, shard)

    def small_copy(step):
        return remote(
            small, small_all.at[shard], small_send.at[step - 1], small_recv.at[step - 1],
            rep, lax.rem(shard + step, plan.shards),
        )

    fewest = jnp.minimum(place, chips - 1 - place)
    longer_above = jnp.where(2 * place < chips - 1, 1, 0)

    def nearest(number):
        inside = number <= 2 * fewest
        above = jnp.where(inside, number % 2, longer_above)
        distance = jnp.where(inside, (number + 1) // 2, number - fewest)
        return place + distance * (2 * above - 1), above

    def hop(mat, origin, down, order, source):
        return remote(
            source,
            slab_part(mat, origin * 2 + core, rep, order),
            z_send.at[mat, origin, down, order],
            z_recv.at[mat, origin, order],
            rep, (place + 1 - 2 * down) * 2 + core,
        )

    def own_hop(mat, down, order):
        return hop(mat, place, down, order, part(own[mat], mat, 0, rep, order))

    def next_hop(mat, number, order):
        origin, above = nearest(number)
        there = slab_part(mat, origin * 2 + core, rep, order)
        return hop(mat, origin, above, order, there)

    def leads(down):
        return (place > 0) if down else (place < chips - 1)

    def goes_on(number):
        _, above = nearest(number)
        onward = place + 1 - 2 * above
        return (onward >= 0) & (onward < chips)

    def along(mat, act):
        for down in range(2):
            @pl.when(leads(down))
            def _(down=down):
                for order in range(plan.orders):
                    act(own_hop(mat, down, order))

    def on(mat, number, act):
        @pl.when(goes_on(number))
        def _():
            for order in range(plan.orders):
                act(next_hop(mat, number, order))

    def give(mat):
        launch(remote(
            own[mat], slab_of(mat, shard), core_send.at[mat, 0], core_recv.at[mat, 0], rep, mate
        ))

    for mat in range(2):
        along(mat, lambda copy: copy.start())
    give(0)
    for step in range(1, plan.shards):
        launch(small_copy(step))
    for mat in range(1, 4):
        give(mat)
    stores = []
    for mat in range(4):
        loads[mat].wait()
        store = pltpu.make_async_copy(stages[mat], slab_of(mat, shard), store_sem.at[mat])
        store.start()
        stores.append(store)

    for fetch in fetches:
        fetch.wait()
    mask_bias[...] = jnp.where(marks[:, 0:1] == segment_across[0:1, :], 0.0, NEG_LARGE)
    angles = marks[:, 1:2].astype(jnp.float32) * rates[0:1, :]
    first = lax.broadcasted_iota(jnp.int32, (1, LANES), 1) % HD < HD // 2
    cosine[...] = jnp.cos(angles)
    sine = jnp.sin(angles)
    before[...] = jnp.where(first, -sine, 0.0)
    after[...] = jnp.where(first, 0.0, sine)

    def source(number):
        return nearest(number)[0] * 2 + core

    def exchange(mat, number, order, step):
        slab = source(number)
        far = plan.flip(rep, plan.ways[order][step])
        at = plan.grow_at(step)
        return [
            remote(
                slab_part(mat, slab, section, order),
                slab_part(mat, slab, section, order),
                rep_send.at[mat, number - 1, order, at + index],
                rep_recv.at[mat, number - 1, order, at + index],
                far, shard,
            )
            for index, section in enumerate(plan.grow(rep, order, step))
        ]

    def await_exchange(mat, number, order, step):
        slab = source(number)
        far = plan.flip(rep, plan.ways[order][step])
        at = plan.grow_at(step)
        for index, section in enumerate(plan.grow(far, order, step)):
            there = slab_part(mat, slab, section, order)
            remote(
                there, there,
                rep_send.at[mat, number - 1, order, at + index],
                rep_recv.at[mat, number - 1, order, at + index],
                far, shard,
            ).wait_recv()

    def relay(mat, number, step):
        for order in range(plan.orders):
            if step == 0:
                origin, _ = nearest(number)
                there = slab_part(mat, origin * 2 + core, rep, order)
                remote(
                    there, there, z_send.at[mat, origin, 0, order], z_recv.at[mat, origin, order],
                    rep, mate,
                ).wait_recv()
            else:
                await_exchange(mat, number, order, step - 1)
            if step < plan.levels:
                for copy in exchange(mat, number, order, step):
                    launch(copy)
        if step == 0:
            on(mat, number, lambda copy: copy.start())
            if number == 1 and mat + 2 < 4:
                along(mat + 2, lambda copy: copy.start())
        if step == plan.levels:
            there = slab_of(mat, source(number))
            launch(remote(
                there, there, core_send.at[mat, number], core_recv.at[mat, number], rep, mate
            ))

    def await_core(mat):
        stores[mat].wait()
        for number in range(chips):
            slab = (place if number == 0 else nearest(number)[0]) * 2 + (1 - core)
            there = slab_of(mat, slab)
            remote(
                there, there, core_send.at[mat, number], core_recv.at[mat, number], rep, mate
            ).wait_recv()

    weight_load = pltpu.make_async_copy(full[0], weight, weight_sem)

    def fetch_weight():
        await_core(0)
        weight_load.start()

    def project():
        weight_load.wait()
        tile = width // 2

        def columns(at):
            span = pl.ds(pl.multiple_of(at * tile, LANES), tile)
            return product(tokens[...], weight[:, span], 1, 0)

        def turned(at, carry):
            joined = columns(at)
            for down in range(tile // LANES):
                vector = joined[:, down * LANES : (down + 1) * LANES]
                spot = pl.ds(pl.multiple_of(lax.rem(at, 2) * tile + down * LANES, LANES), LANES)
                low = (
                    vector * cosine[...]
                    + pltpu.roll(vector, LANES - HD // 2, 1) * before[...]
                    + pltpu.roll(vector, HD // 2, 1) * after[...]
                ).astype(jnp.bfloat16)

                @pl.when(at < 2)
                def _():
                    query[:, spot] = low

                @pl.when(at >= 2)
                def _():
                    key[:, spot] = low
            return carry

        lax.fori_loop(0, 4, turned, 0)

        def plain(at, carry):
            value[:, pl.ds(pl.multiple_of(at * tile, LANES), tile)] = columns(at + 4).astype(
                jnp.bfloat16
            )
            return carry

        lax.fori_loop(0, 2, plain, 0)

    def attend(low, high):
        def one(pair, carry):
            forward_pair(pair, query, key, value, mask_bias, attended, logsum)
            return carry

        lax.fori_loop(low, high, one, 0)

    copies = [
        pltpu.make_async_copy(here, far, result_sem.at[at])
        for at, (here, far) in enumerate(zip(near, results))
    ]

    def mix():
        def one(at, carry):
            span = pl.ds(pl.multiple_of(at * 256, 256), 256)
            across = pl.ds(pl.multiple_of(3 * width + at * 256, 256), 256)
            inner_resid[:, span] = tokens[:, span].astype(jnp.float32) + product(
                attended[...], weight[:, across], 1, 0
            )
            return carry

        lax.fori_loop(0, width // 256, one, 0)
        for copy in copies:
            copy.start()

    items = [(mat, number) for mat in range(4) for number in range(1, chips)]
    events = [
        (at + SLACK * step, -step, functools.partial(relay, *item, step))
        for at, item in enumerate(items)
        for step in range(plan.levels + 1)
    ]
    ready = chips - 1 + SLACK * plan.levels
    for late, work in (
        (0, fetch_weight),
        (1, project),
        (2, functools.partial(attend, 0, pairs // 2)),
        (3, functools.partial(attend, pairs // 2, pairs)),
        (4, mix),
    ):
        events.append((ready + late, 1, work))
    for _, _, event in sorted(events, key=lambda event: event[:2]):
        event()

    for mat in range(1, 4):
        await_core(mat)
    for step in range(1, plan.shards):
        small_copy(step).wait_recv()
    for copy in sent:
        copy.wait_send()
    for mat in range(4):
        along(mat, lambda copy: copy.wait_send())
        for number in range(1, chips):
            on(mat, number, lambda copy: copy.wait_send())
    for copy in copies:
        copy.wait()


def gather_weights(plan, own, small, carried):
    hbm = pl.BlockSpec(memory_space=pl.ANY)
    vmem = pl.BlockSpec(memory_space=pltpu.VMEM)
    dma = pltpu.SemaphoreType.DMA
    shapes = [
        jax.ShapeDtypeStruct((array.shape[0] * plan.shards, array.shape[1]), array.dtype)
        for array in own
    ]
    gaps = plan.chips - 1
    crossing = plan.replicas - 1
    length, width = carried[0].shape
    wide, low = jnp.float32, jnp.bfloat16
    results = (
        [jax.ShapeDtypeStruct((length, width), low)] * 4
        + [
            jax.ShapeDtypeStruct((width // HD, length), wide),
            jax.ShapeDtypeStruct((length, width), wide),
        ]
        + [jax.ShapeDtypeStruct((length, LANES), wide)] * 3
    )
    return pl.pallas_call(
        functools.partial(gather_kernel, plan),
        out_shape=shapes + [jax.ShapeDtypeStruct((plan.shards,) + small.shape, small.dtype)]
        + results,
        in_specs=[hbm] * 4 + [vmem] + [hbm] * len(carried),
        out_specs=[hbm] * 4 + [vmem] + [hbm] * len(results),
        scratch_shapes=[pltpu.VMEM(array.shape, array.dtype) for array in own]
        + [
            dma((4,)),
            dma((4,)),
            dma((plan.shards - 1,)),
            dma((plan.shards - 1,)),
            dma((4, plan.chips, 2, plan.orders)),
            dma((4, plan.chips, plan.orders)),
            dma((4, gaps, plan.orders, crossing)),
            dma((4, gaps, plan.orders, crossing)),
            dma((4, plan.chips)),
            dma((4, plan.chips)),
        ]
        + [pltpu.VMEM(array.shape, array.dtype) for array in carried]
        + [pltpu.VMEM(result.shape, result.dtype) for result in results]
        + [
            pltpu.VMEM(shapes[0].shape, low),
            pltpu.VMEM((length, length), wide),
            dma((len(carried),)),
            dma,
            dma((len(results),)),
        ],
        compiler_params=pltpu.CompilerParams(
            collective_id=0, has_side_effects=True, vmem_limit_bytes=VMEM_LIMIT
        ),
        name="gather_weights",
    )(*own, small, *carried)


def back_pair(pair, query, key, value, upper, logsum, mask_bias, tables, joined_low, width):
    length = query.shape[0]
    block = min(length, 256)
    span = pl.ds(pl.multiple_of(pair * LANES, LANES), LANES)
    lane = lax.broadcasted_iota(jnp.int32, (1, LANES), 1)
    keys, values = key[:, span], value[:, span]
    query_parts = [0.0] * (length // block)
    key_total = value_total = 0.0
    for half in range(LANES // HD):
        pick = jnp.where(lane // HD == half, 1.0, 0.0).astype(jnp.bfloat16)
        scaled = pick * jnp.bfloat16(1.0 / math.sqrt(HD))
        keys_scaled = keys * scaled
        rowsum = logsum[pl.ds(pair * (LANES // HD) + half, 1), :]
        for at in range(length // block):
            rows = slice(at * block, (at + 1) * block)
            queries_scaled = query[rows, span] * scaled
            grads = upper[rows, span] * pick
            scores = product(keys, queries_scaled, 1, 1) + mask_bias[:, rows]
            probs = jnp.exp(scores - rowsum[:, rows])
            dprobs = product(values, grads, 1, 1)
            dots = jnp.sum(probs * dprobs, axis=0, keepdims=True)
            score_grad = (probs * (dprobs - dots)).astype(jnp.bfloat16)
            value_total += product(probs.astype(jnp.bfloat16), grads, 1, 0)
            key_total += product(score_grad, queries_scaled, 1, 0)
            query_parts[at] += product(score_grad, keys_scaled, 0, 0)
    cosine, before, after = tables

    def unrotate(grad, rows):
        return (
            grad * cosine[rows, :]
            - pltpu.roll(grad, LANES - HD // 2, 1) * before[rows, :]
            - pltpu.roll(grad, HD // 2, 1) * after[rows, :]
        ).astype(jnp.bfloat16)

    for at, part in enumerate(query_parts):
        rows = slice(at * block, (at + 1) * block)
        joined_low[rows, span] = unrotate(part, rows)
    everything = slice(0, length)
    joined_low[:, pl.ds(pl.multiple_of(width + pair * LANES, LANES), LANES)] = unrotate(
        key_total, everything
    )
    joined_low[:, pl.ds(pl.multiple_of(2 * width + pair * LANES, LANES), LANES)] = (
        value_total.astype(jnp.bfloat16)
    )


def sum_kernel(plan, *refs):
    mixing, gate, up, down, small = refs[:5]
    carried, weight = refs[5:17], refs[17]
    outs, small_out, input_grad = refs[18:22], refs[22], refs[23]
    (held, mate_in, rep_in, z_in, final, small_in, load_sem, out_sem, small_sem, mate_send,
     mate_recv, rep_send, rep_recv, z_send, z_recv, last_send, last_recv) = refs[24:41]
    here, weight_here = refs[41:53], refs[53]
    joined_low, joined, mask_bias, tokens_across, fetch_sem, result_sem = refs[54:60]
    result_here = refs[60]
    rep, shard = lax.axis_index("rep"), lax.axis_index("shard")
    chips, piece, levels = plan.chips, plan.piece, plan.levels
    place, core = lax.div(shard, 2), lax.rem(shard, 2)
    mate = place * 2 + (1 - core)
    rows = held.shape[2]
    total = plan.replicas * plan.shards
    early = 3 * chips
    count = 4 * chips
    (query, key, value, upper, logsum, segment_down, segment_across, cosine, before, after, tokens,
     inner_grad) = here
    width = query.shape[1]
    pairs = width // LANES

    def fragments(turn, slab):
        top = pl.multiple_of(slab * rows, 8)
        if turn == 3:
            wide = joined.shape[1]
            return [
                (joined.at[pl.ds(top, rows), :], 0, wide),
                (mixing.at[pl.ds(top, rows), :], wide, mixing.shape[1]),
            ]
        if turn > 0:
            return [((gate, up)[turn - 1].at[pl.ds(top, rows), :], 0, plan.width)]
        wide = down.shape[1]
        return [
            (
                down.at[
                    pl.ds(pl.multiple_of(slab * (rows * (plan.width // wide)) + at * rows, 8), rows),
                    :,
                ],
                at * wide,
                wide,
            )
            for at in range(plan.width // wide)
        ]

    gaps = list(range(1, chips)) + [0]

    def slab_at(gap, which):
        return lax.rem(place + gap, chips) * 2 + which

    def load(turn):
        for gap in gaps:
            for ref, left, wide in fragments(turn, slab_at(gap, core)):
                pltpu.make_async_copy(
                    ref, held.at[turn, gap, :, pl.ds(left, wide)], load_sem.at[turn, gap]
                ).start()

    def give(turn):
        for gap in gaps:
            for ref, left, wide in fragments(turn, slab_at(gap, 1 - core)):
                remote(
                    ref, mate_in.at[turn, gap, :, pl.ds(left, wide)],
                    mate_send.at[turn, gap], mate_recv.at[turn, gap], rep, mate,
                ).start()

    for turn in range(3):
        load(turn)
    fetches = [
        pltpu.make_async_copy(far, near, fetch_sem.at[at])
        for at, (far, near) in enumerate(zip(carried, here))
    ]
    fetches.append(
        pltpu.make_async_copy(
            weight.at[:, pl.ds(0, 3 * width)], weight_here, fetch_sem.at[len(carried)]
        )
    )
    for fetch in fetches:
        fetch.start()
    greet_all(plan, rep, shard)
    for turn in range(3):
        give(turn)

    def small_go(step, carry):
        other = lax.rem(rep * plan.shards + shard + step, total)
        other_rep, other_shard = lax.div(other, plan.shards), lax.rem(other, plan.shards)
        remote(
            small.at[other_shard], small_in.at[step - 1], small_sem.at[0], small_sem.at[1],
            other_rep, other_shard,
        ).start()
        return carry

    lax.fori_loop(1, total, small_go, 0)

    def whole_mate(turn, gap):
        return remote(
            mate_in.at[turn, gap], mate_in.at[turn, gap],
            mate_send.at[turn, gap], mate_recv.at[turn, gap], rep, mate,
        )

    def cross(turn, gap, order, step):
        far = plan.flip(rep, plan.ways[order][step])
        at = plan.halve_at(step)
        copies = [
            remote(
                held.at[turn, gap, :, pl.ds(plan.column(section, order), piece)],
                rep_in.at[turn, gap, order, at + number],
                rep_send.at[turn, gap, order, at + number],
                rep_recv.at[turn, gap, order, at + number],
                far, shard,
            )
            for number, section in enumerate(plan.halve(far, order, step))
        ]
        return copies, [plan.column(section, order) for section in plan.halve(rep, order, step)]

    wide_piece = plan.orders * piece
    own_columns = pl.ds(pl.multiple_of(rep * wide_piece, LANES), wide_piece)

    def z_copy(turn, gap):
        return remote(
            held.at[turn, gap, :, own_columns],
            z_in.at[turn, gap - 1],
            z_send.at[turn, gap - 1], z_recv.at[turn, gap - 1],
            rep, slab_at(gap, core),
        )

    def item_of(number):
        return lax.div(number, chips), lax.rem(lax.rem(number, chips) + 1, chips)

    def advance(number, step):
        turn, gap = item_of(number)
        if step == 0:
            pltpu.make_async_copy(
                held.at[turn, gap], held.at[turn, gap], load_sem.at[turn, gap]
            ).wait()
            whole_mate(turn, gap).wait_recv()

            def add(at, carry):
                span = pl.ds(pl.multiple_of(at * piece, LANES), piece)
                held[turn, gap, :, span] = (
                    held[turn, gap, :, span].astype(jnp.float32)
                    + mate_in[turn, gap, :, span].astype(jnp.float32)
                ).astype(jnp.bfloat16)
                return carry

            lax.fori_loop(0, plan.width // piece, add, 0)
        else:
            for order in range(plan.orders):
                copies, columns = cross(turn, gap, order, step - 1)
                at = plan.halve_at(step - 1)
                for index, (copy, column) in enumerate(zip(copies, columns)):
                    copy.wait_recv()
                    span = pl.ds(column, piece)
                    held[turn, gap, :, span] = (
                        held[turn, gap, :, span].astype(jnp.float32)
                        + rep_in[turn, gap, order, at + index].astype(jnp.float32)
                    ).astype(jnp.bfloat16)
        if step < levels:
            for order in range(plan.orders):
                for copy in cross(turn, gap, order, step)[0]:
                    copy.start()
        else:
            @pl.when(gap > 0)
            def _():
                z_copy(turn, gap).start()

    def spread(turn, order, step):
        far = plan.flip(rep, plan.ways[order][step])
        at = plan.grow_at(step)
        return [
            remote(
                final.at[turn, :, pl.ds(plan.column(section, order), piece)],
                final.at[turn, :, pl.ds(plan.column(section, order), piece)],
                last_send.at[turn, order, at + number],
                last_recv.at[turn, order, at + number],
                far, shard,
            )
            for number, section in enumerate(plan.grow(rep, order, step))
        ]

    def await_spread(turn, order, step):
        far = plan.flip(rep, plan.ways[order][step])
        at = plan.grow_at(step)
        for number, section in enumerate(plan.grow(far, order, step)):
            there = final.at[turn, :, pl.ds(plan.column(section, order), piece)]
            remote(
                there, there,
                last_send.at[turn, order, at + number],
                last_recv.at[turn, order, at + number],
                far, shard,
            ).wait_recv()

    def finish(turn, step):
        if step == 0:
            for gap in range(1, chips):
                z_copy(turn, gap).wait_recv()
            for order in range(plan.orders):
                span = pl.ds(plan.column(rep, order), piece)
                part = pl.ds(order * piece, piece)
                value = held[turn, 0, :, span].astype(jnp.float32)
                for gap in range(1, chips):
                    value = value + z_in[turn, gap - 1, :, part].astype(jnp.float32)
                final[turn, :, span] = value.astype(jnp.bfloat16)
        else:
            for order in range(plan.orders):
                await_spread(turn, order, step - 1)
        if step < levels:
            for order in range(plan.orders):
                for copy in spread(turn, order, step):
                    copy.start()

    def tick(now):
        for step in reversed(range(levels + 1)):
            late = now - (SLACK * (levels + step + 1) + chips - 1)

            @pl.when((late >= 0) & (lax.rem(late + chips, chips) == 0) & (late < count))
            def _(late=late, step=step):
                finish(lax.div(late, chips), step)

        for step in reversed(range(levels + 1)):
            number = now - SLACK * step

            @pl.when((number >= 0) & (number < count))
            def _(number=number, step=step):
                advance(number, step)

    tick(0)
    for fetch in fetches:
        fetch.wait()
    mask_bias[...] = jnp.where(segment_down[:, 0:1] == segment_across[0:1, :], 0.0, NEG_LARGE)

    def attend(now, carry):
        @pl.when(now < pairs)
        def _():
            back_pair(
                now, query, key, value, upper, logsum, mask_bias, (cosine, before, after),
                joined_low, width,
            )

        @pl.when(now + 1 < early)
        def _():
            tick(now + 1)
        return carry

    lax.fori_loop(0, max(pairs, early - 1), attend, 0)
    tokens_across[...] = tokens[...].T

    def weigh(at, carry):
        span = pl.ds(pl.multiple_of(at * (width // 2), LANES), width // 2)
        joined[:, span] = product(tokens_across[...], joined_low[:, span], 1, 0).astype(
            jnp.bfloat16
        )
        return carry

    lax.fori_loop(0, 6, weigh, 0)
    load(3)
    give(3)

    def back(at, carry):
        low = pl.ds(pl.multiple_of(at * 256, 256), 256)
        result_here[:, low] = (
            inner_grad[:, low] + product(joined_low[...], weight_here[low, :], 1, 1)
        ).astype(jnp.bfloat16)
        return carry

    lax.fori_loop(0, width // 256, back, 0)
    result_copy = pltpu.make_async_copy(result_here, input_grad, result_sem)
    result_copy.start()

    def late_tick(now, carry):
        tick(now)
        return carry

    lax.fori_loop(early, count + SLACK * (2 * levels + 1), late_tick, 0)

    everything = remote(small_in, small_in, small_sem.at[0], small_sem.at[1], rep, mate)
    everything.wait_recv()

    def gain(at, value):
        return value + small_in[at]

    small_out[...] = lax.fori_loop(0, total - 1, gain, small[shard])
    everything.wait_send()
    for turn in range(4):
        pltpu.make_async_copy(final.at[turn], outs[turn], out_sem.at[turn]).start()

    def drain(number, carry):
        turn, gap = item_of(number)
        whole_mate(turn, gap).wait_send()
        for order in range(plan.orders):
            for step in range(levels):
                for copy in cross(turn, gap, order, step)[0]:
                    copy.wait_send()

        @pl.when(gap > 0)
        def _():
            z_copy(turn, gap).wait_send()
        return carry

    lax.fori_loop(0, count, drain, 0)
    for turn in range(4):
        for order in range(plan.orders):
            for step in range(levels):
                for copy in spread(turn, order, step):
                    copy.wait_send()
        pltpu.make_async_copy(final.at[turn], outs[turn], out_sem.at[turn]).wait()
    result_copy.wait()


def sum_grads(plan, grads, small, carried, weight):
    hbm = pl.BlockSpec(memory_space=pl.ANY)
    vmem = pl.BlockSpec(memory_space=pltpu.VMEM)
    dma = pltpu.SemaphoreType.DMA
    chips, gaps, crossing = plan.chips, plan.chips - 1, plan.replicas - 1
    rows = grads[0].shape[0] // plan.shards
    low = jnp.bfloat16
    total = plan.replicas * plan.shards
    length, width = carried[0].shape
    return pl.pallas_call(
        functools.partial(sum_kernel, plan),
        out_shape=[jax.ShapeDtypeStruct((rows, plan.width), low)] * 4
        + [
            jax.ShapeDtypeStruct(small.shape[1:], small.dtype),
            jax.ShapeDtypeStruct((length, width), low),
        ],
        in_specs=[hbm] * 4 + [vmem] + [hbm] * (len(carried) + 1),
        out_specs=[hbm] * 4 + [vmem, hbm],
        scratch_shapes=[
            pltpu.VMEM((4, chips, rows, plan.width), low),
            pltpu.VMEM((4, chips, rows, plan.width), low),
            pltpu.VMEM((4, chips, plan.orders, crossing, rows, plan.piece), low),
            pltpu.VMEM((4, gaps, rows, plan.orders * plan.piece), low),
            pltpu.VMEM((4, rows, plan.width), low),
            pltpu.VMEM((total - 1,) + small.shape[1:], small.dtype),
            dma((4, chips)),
            dma((4,)),
            dma((2,)),
            dma((4, chips)),
            dma((4, chips)),
            dma((4, chips, plan.orders, crossing)),
            dma((4, chips, plan.orders, crossing)),
            dma((4, gaps)),
            dma((4, gaps)),
            dma((4, plan.orders, crossing)),
            dma((4, plan.orders, crossing)),
        ]
        + [pltpu.VMEM(array.shape, array.dtype) for array in carried]
        + [
            pltpu.VMEM((width, 3 * width), low),
            pltpu.VMEM((length, 3 * width), low),
            pltpu.VMEM((width, 3 * width), low),
            pltpu.VMEM((length, length), jnp.float32),
            pltpu.VMEM((width, length), low),
            dma((len(carried) + 1,)),
            dma,
            pltpu.VMEM((length, width), low),
        ],
        compiler_params=pltpu.CompilerParams(
            collective_id=1, has_side_effects=True, vmem_limit_bytes=VMEM_LIMIT
        ),
        name="sum_grads",
    )(*grads, small, *carried, weight)


def layer_norm(values, gain, shift):
    centred = values - jnp.mean(values, axis=-1, keepdims=True)
    variance = jnp.mean(centred * centred, axis=-1, keepdims=True)
    return centred * lax.rsqrt(variance + EPSILON) * gain + shift


def transposed_product(left, right):
    return lax.dot_general(
        left, right, (((1,), (1,)), ((), ())), preferred_element_type=jnp.float32
    )


def token_contract(left, right):
    return lax.dot_general(
        left, right, (((0,), (0,)), ((), ())), preferred_element_type=jnp.float32
    )


def on_device(
    tokens,
    joined_weight,
    mixing_weight,
    gate_weight,
    up_weight,
    down_weight,
    inner_gain,
    inner_shift,
    outer_gain,
    outer_shift,
    segments,
    positions,
    cotangent,
):
    replicas, shards = lax.axis_size("rep"), lax.axis_size("shard")
    plan = Plan(gate_weight.shape[1], replicas, shards)
    part_rows = joined_weight.shape[0]
    own_vectors = jnp.stack([inner_gain, inner_shift, outer_gain, outer_shift]).astype(jnp.float32)
    own_vectors = jnp.pad(own_vectors, ((0, 4), (0, LANES - part_rows)))
    length, model_width = tokens.shape
    halves = np.arange(LANES) % (HD // 2)
    rates = np.float32(1000.0) ** (-(2.0 * halves.astype(np.float32)) / np.float32(HD))
    marks = jnp.where(
        jnp.arange(LANES)[None, :] == 0, segments[0][:, None], positions[0][:, None]
    )
    (
        attention_full,
        gate_full,
        upward_full,
        down_full,
        vectors,
        query_low,
        key_low,
        value_low,
        attended_low,
        logsum,
        inner_resid,
        cosine_wide,
        before,
        after,
    ) = gather_weights(
        plan,
        (
            jnp.concatenate([joined_weight, mixing_weight], axis=1),
            gate_weight,
            up_weight,
            down_weight,
        ),
        own_vectors,
        (tokens, marks, segments, jnp.asarray(np.tile(rates[None, :], (8, 1)))),
    )
    mixing_full = attention_full[:, joined_weight.shape[1] :]
    vectors = vectors[:, :4, :part_rows].transpose(1, 0, 2).reshape(4, shards * part_rows)
    innergain_full, innershift_full, outergain_full, outershift_full = vectors
    normed, inner_pull = jax.vjp(
        layer_norm,
        inner_resid,
        innergain_full.astype(jnp.float32),
        innershift_full.astype(jnp.float32),
    )
    normed_low = normed.astype(jnp.bfloat16)
    gate_rows = jnp.dot(normed_low, gate_full, preferred_element_type=jnp.float32)
    upward = jnp.dot(normed_low, upward_full, preferred_element_type=jnp.float32)
    active, silu_pull = jax.vjp(
        lambda first, second: jax.nn.silu(first) * second, gate_rows, upward
    )
    active_low = active.astype(jnp.bfloat16)
    result = jnp.dot(active_low, down_full, preferred_element_type=jnp.float32)
    final, outer_pull = jax.vjp(
        layer_norm,
        normed + result,
        outergain_full.astype(jnp.float32),
        outershift_full.astype(jnp.float32),
    )
    layer_output = final.astype(jnp.bfloat16)
    gate_back, upward_back, down_back = gate_full, upward_full, down_full
    outer_grad, outergain_grad, outershift_grad = outer_pull(cotangent.astype(jnp.float32))
    result_grad = outer_grad.astype(jnp.bfloat16)
    down_grad = token_contract(active_low, result_grad)
    active_grad = transposed_product(result_grad, down_back)
    gate_part, upward_part = silu_pull(active_grad)
    gate_low = gate_part.astype(jnp.bfloat16)
    upward_low = upward_part.astype(jnp.bfloat16)
    gate_grad = token_contract(normed_low, gate_low)
    up_grad = token_contract(normed_low, upward_low)
    normed_grad = (
        outer_grad
        + transposed_product(gate_low, gate_back)
        + transposed_product(upward_low, upward_back)
    )
    inner_grad, innergain_grad, innershift_grad = inner_pull(normed_grad)
    mixing_back = mixing_full
    branch_grad = inner_grad.astype(jnp.bfloat16)
    mixing_grad = token_contract(attended_low, branch_grad)
    attended_grad = transposed_product(branch_grad, mixing_back).astype(jnp.bfloat16)

    small = jnp.stack([innergain_grad, innershift_grad, outergain_grad, outershift_grad])
    small = small.reshape(4, shards, part_rows).transpose(1, 0, 2)
    small = jnp.pad(small, ((0, 0), (0, 4), (0, LANES - part_rows)))
    low = jnp.bfloat16
    down_sum, gate_sum, up_sum, attention_sum, small_sum, input_grad = sum_grads(
        plan,
        (mixing_grad.astype(low), gate_grad.astype(low), up_grad.astype(low), down_grad.astype(low)),
        small,
        (
            query_low,
            key_low,
            value_low,
            attended_grad,
            logsum,
            marks,
            segments,
            cosine_wide,
            before,
            after,
            tokens,
            inner_grad,
        ),
        attention_full,
    )
    down_sum = down_sum.reshape(part_rows, -1, model_width).transpose(1, 0, 2)
    full = jnp.float32
    return (
        layer_output,
        input_grad,
        attention_sum[:, : joined_weight.shape[1]].astype(full),
        attention_sum[:, joined_weight.shape[1] :].astype(full),
        gate_sum.astype(full),
        up_sum.astype(full),
        down_sum.reshape(down_weight.shape).astype(full),
        small_sum[0, :part_rows],
        small_sum[1, :part_rows],
        small_sum[2, :part_rows],
        small_sum[3, :part_rows],
    )


def solution(mesh):
    placed = (
        P(("rep", "shard"), None),
        P("shard", None),
        P("shard", None),
        P("shard", None),
        P("shard", None),
        P("shard", None),
        P("shard"),
        P("shard"),
        P("shard"),
        P("shard"),
        P(("rep", "shard"), None),
        P(("rep", "shard"), None),
        P(("rep", "shard"), None),
    )
    return jax.shard_map(
        on_device,
        mesh=mesh,
        in_specs=placed,
        out_specs=(
            P(("rep", "shard"), None),
            P(("rep", "shard"), None),
            P("shard", None),
            P("shard", None),
            P("shard", None),
            P("shard", None),
            P("shard", None),
            P("shard"),
            P("shard"),
            P("shard"),
            P("shard"),
        ),
        check_vma=False,
    )
```

profile of v0, /device:TPU:0, one launch (start us, length us, event | category | flops | bytes accessed | tf_op | source)
XLA Modules:
  0.0 267.6 jit_solution(11559896141099075526)
XLA Ops:
  0.7 1.3 fusion.21.refs_4_
  2.0 1.6 broadcast_select_fusion.refs_6_.refs_10_
  3.6 2.0 pad_maximum_fusion.refs_0_
  5.5 82.4 %gather_weights.1 = (bf16[768,3072]{1,0:T(8,128)(2,1)}, bf16[768,3072]{1,0:T(8,128)(2,1)}, bf16[768,3072]{1,0:T(8,128)(2,1)}, bf16[3072,768]{1,0:T(8,128)(2,1)},...) custom-call(bf16[96,3072]{1,0:T(8,128)(2,1)} %pad_maximum_fusion.ref, ...), custom_call_target="tpu_custom_call" | custom-call | tf_op jit(solution)/shard_map/gather_weights/pallas_call | solution.py:465
  88.0 0.0 copy-start
  88.0 0.9 slice_bitcast_fusion
  88.9 0.1 slice_reduce_fusion.1
  88.9 0.1 mul.150
  89.0 1.6 reduce_sum.105
  90.6 0.0 copy-done
  90.6 0.3 multiply_reduce_fusion.3
  90.9 0.1 mul.142
  90.9 0.1 add.58
  91.0 0.1 add.64
  91.1 0.3 fusion.8
  91.4 0.0 copy-start.4
  91.4 0.0 slice-start.3
  91.4 0.0 slice-start.6
  91.4 4.9 %fusion.31 = f32[512,3072]{1,0:T(8,128)S(1)} fusion(bf16[512,768]{1,0:T(8,128)(2,1)S(1)} %fusion.8, bf16[768,3072]{1,0:T(8,128)(2,1)} %get-tuple-element.33), kind=kOutput, calls=%fused_computation.80 | convolution fusion | flops 2415919104 | bytes 11796480 | tf_op jit(solution)/shard_map/dot_general | solution.py:989
  96.4 0.0 copy-done.4
  96.4 0.0 slice-done.2
  96.4 0.0 slice-start.7
  96.4 4.9 %multiply_convert_fusion.1 = (bf16[512,3072]{1,0:T(8,128)(2,1)S(1)}, f32[512,3072]{1,0:T(8,128)}) fusion(f32[512,3072]{1,0:T(8,128)S(1)} %fusion.31, bf16[512,768]{1,0:T(8,128)(2,1)S(1)} %fusion.8, bf16[768,3072]{1,0:T(8,128)(2,1)S(1)} %bitcast.48), kind=kOutput, calls=%fused_computation.5 | convolution fusion | flops 2425356288 | bytes 21233664 | tf_op jit(solution)/shard_map/dot_general | solution.py:990
  101.4 0.0 copy-done.2
  101.4 0.0 slice-done.6
  101.4 0.0 slice-done.7
  101.4 2.7 %fusion.30 = (f32[512]{0:T(512)S(1)}, f32[512,768]{1,0:T(8,128)S(1)}) fusion(bf16[512,3072]{1,0:T(8,128)(2,1)S(1)} %get-tuple-element.72, bf16[3072,768]{1,0:T(8,128)(2,1)S(1)} %bitcast.52, f32[768]{0:T(1024)S(1)} %add.58, f32[768]{0:T(1024)S(1)} %mul.142, f32[512]{0:T(512)S(1)} %fusion.25, f32[512,768]{1,0:T(8,128)S(1)} %copy-done, ...), kind=kOutput, calls=%fused_computation.79 | convolution fusion | flops 2418277888 | bytes 11022336 | tf_op jit(solution)/shard_map/dot_general | solution.py:995
  104.2 0.0 copy-done.15
  104.2 0.0 copy-start.3
  104.2 0.3 multiply_reduce_fusion.2
  104.5 0.8 copy-done.3
  105.3 0.7 fusion.7
  106.0 0.1 stack.37
  106.1 0.1 stack.38
  106.2 0.0 slice-start.4
  106.2 2.9 %fusion.29 = (f32[512]{0:T(512)S(1)}, f32[512,768]{1,0:T(8,128)S(1)}, bf16[512,768]{1,0:T(8,128)(2,1)}) fusion(f32[512]{0:T(512)S(1)} %multiply_multiply_fusion.1, f32[512,768]{1,0:T(8,128)S(1)} %get-tuple-element.75, f32[512]{0:T(512)S(1)} %broadcast_multiply_fusion, f32[512]{0:T(512)S(1)} %fusion.26, f32[768]{0:T(1024)S(1)} %mul.150, ...), kind=kLoop, calls=%fused_computation.78 | loop fusion | flops 4718080 | bytes 4732928 | tf_op jit(solution)/shard_map/transpose(jvp())/reduce_sum | solution.py:910
  109.0 8.5 %multiply_convert_fusion = (bf16[512,3072]{1,0:T(8,128)(2,1)S(1)}, bf16[512,3072]{1,0:T(8,128)(2,1)S(1)}) fusion(f32[512,3072]{1,0:T(8,128)} %copy-done.2, f32[512,3072]{1,0:T(8,128)} %get-tuple-element.73, bf16[3072,768]{1,0:T(8,128)(2,1)} %get-tuple-element.35, f32[512,768]{1,0:T(8,128)S(1)} %get-tuple-element.64, f32[512]{0:T(512)S(1)} %negate_multiply_fusion.1), kind=kOutput, calls=%fused_computation.4 | convolution fusion | flops 2438725632 | bytes 25167872 | tf_op jit(solution)/shard_map/dot_general | solution.py:916
  117.6 2.7 fusion.32
  120.4 3.2 %multiply_reduce_fusion = (f32[768]{0:T(1024)S(1)}, f32[512]{0:T(512)S(1)}, f32[768]{0:T(1024)S(1)}, f32[512,768]{1,0:T(8,128)S(1)}) fusion(f32[512,768]{1,0:T(8,128)S(1)} %copy-done, f32[512]{0:T(512)S(1)} %fusion.25, f32[512]{0:T(512)S(1)} %broadcast_multiply_fusion.1, f32[768]{0:T(1024)S(1)} %mul.142, bf16[512,3072]{1,0:T(8,128)(2,1)S(1)} %get-tuple-element.65, ...), kind=kOutput, calls=%fused_computation.20 | convolution fusion | flops 2420242432 | bytes 14173184 | tf_op jit(solution)/shard_map/dot_general | solution.py:916
  123.6 4.4 %convolution_convert_fusion.refs_3_ = bf16[3072,768]{1,0:T(8,128)(2,1)} fusion(bf16[512,3072]{1,0:T(8,128)(2,1)S(1)} %copy-done.16, f32[512,768]{1,0:T(8,128)S(1)} %get-tuple-element.64, f32[512]{0:T(512)S(1)} %negate_multiply_fusion.1), kind=kOutput, calls=%fused_computation.8 | convolution fusion | flops 2419064832 | bytes 9439232 | tf_op jit(solution)/shard_map/dot_general | solution.py:922
  128.0 0.1 stack.35
  128.1 0.6 fusion.28
  128.8 0.2 broadcast_add_fusion.refs_16_
  128.9 0.0 copy-start.1
  128.9 0.1 stack.36
  129.1 0.6 pad.12.refs_4_
  129.7 0.3 copy-done.6
  130.0 1.8 convolution_convert_fusion.3.refs_0_
  131.8 3.0 %convolution_convert_fusion.4.refs_8_ = bf16[512,768]{1,0:T(8,128)(2,1)} fusion(bf16[768,3072]{1,0:T(8,128)(2,1)} %get-tuple-element.40.refs_17_, f32[512,768]{1,0:T(8,128)S(1)} %broadcast_add_fusion.refs_16_), kind=kOutput, calls=%fused_computation.30 | convolution fusion | flops 604766208 | bytes 3538944 | tf_op jit(solution)/shard_map/dot_general | solution.py:916
  134.8 0.0 copy-done.5
  134.9 4.4 %convolution_convert_fusion.1.refs_2_ = bf16[768,3072]{1,0:T(8,128)(2,1)} fusion(bf16[512,768]{1,0:T(8,128)(2,1)S(1)} %copy-done.5, bf16[512,3072]{1,0:T(8,128)(2,1)S(1)} %copy-done.14), kind=kOutput, calls=%fused_computation.9 | convolution fusion | flops 2418278400 | bytes 8650752 | tf_op jit(solution)/shard_map/dot_general | solution.py:922
  139.3 4.4 %convolution_convert_fusion.2.refs_1_ = bf16[768,3072]{1,0:T(8,128)(2,1)} fusion(bf16[512,768]{1,0:T(8,128)(2,1)S(1)} %copy-done.5, bf16[512,3072]{1,0:T(8,128)(2,1)S(1)} %copy-done.12), kind=kOutput, calls=%fused_computation.10 | convolution fusion | flops 2418278400 | bytes 8650752 | tf_op jit(solution)/shard_map/dot_general | solution.py:922
  143.7 113.9 %sum_grads.1 = (bf16[96,3072]{1,0:T(8,128)(2,1)}, bf16[96,3072]{1,0:T(8,128)(2,1)}, bf16[96,3072]{1,0:T(8,128)(2,1)}, bf16[96,3072]{1,0:T(8,128)(2,1)}, f32[8,128]{1,0:T(8,128)}, /*index=5*/bf16[512,768]{1,0:T(8,128)(2,1)}) custom-call(bf16[768,768]{1,0:T(8,128)(2,1)} %convolution_convert_fusion.3.refs_0_, ...), custom_call_target="tpu_custom_call" | custom-call | tf_op jit(solution)/shard_map/sum_grads/pallas_call | solution.py:863
  257.6 0.0 copy-start.10
  257.6 1.4 slice_bitcast_fusion.1
  258.9 1.6 slice_convert_fusion.1
  260.6 2.0 slice_convert_fusion
  262.6 0.0 copy-done.10
  262.6 1.1 convert_element_type.83
  263.8 1.1 convert_element_type.84
  264.9 0.6 reshape.114
  265.4 0.0 copy-start.7
  265.5 1.2 copy.25
  266.7 0.9 copy.27
  (43 shorter events, 0.1 us)
Async XLA Ops:
  88.0 2.6 copy-start
  91.1 5.3 %slice-start.2 = ((s8[4718592]{0:T(1024)(128)(4,1)}), s8[4194304]{0:T(1024)(128)(4,1)S(1)}, s32[]{:S(2)}) async-start(s8[4718592]{0:T(1024)(128)(4,1)} %bitcast.47), calls=%async_computation.2 | async-start | bytes 8388608
  91.4 5.0 %copy-start.4 = (bf16[512,768]{1,0:T(8,128)(2,1)}, bf16[512,768]{1,0:T(8,128)(2,1)S(1)}, u32[]{:S(2)}) copy-start(bf16[512,768]{1,0:T(8,128)(2,1)S(1)} %fusion.8) | copy-start | bytes 2359300
  91.4 5.0 %slice-start.3 = ((s8[4718592]{0:T(1024)(128)(4,1)}), s8[524288]{0:T(1024)(128)(4,1)S(1)}, s32[]{:S(2)}) async-start(s8[4718592]{0:T(1024)(128)(4,1)} %bitcast.47), calls=%async_computation.3 | async-start | bytes 1048576
  91.4 10.0 %slice-start.6 = ((s8[4718592]{0:T(1024)(128)(4,1)}), s8[4194304]{0:T(1024)(128)(4,1)S(1)}, s32[]{:S(2)}) async-start(s8[4718592]{0:T(1024)(128)(4,1)} %bitcast.51), calls=%async_computation.6 | async-start | bytes 8388608
  96.4 5.0 %copy-start.2 = (f32[512,3072]{1,0:T(8,128)}, f32[512,3072]{1,0:T(8,128)S(1)}, u32[]{:S(2)}) copy-start(f32[512,3072]{1,0:T(8,128)S(1)} %fusion.31) | copy-start | bytes 18874372
  96.4 5.0 %slice-start.7 = ((s8[4718592]{0:T(1024)(128)(4,1)}), s8[524288]{0:T(1024)(128)(4,1)S(1)}, s32[]{:S(2)}) async-start(s8[4718592]{0:T(1024)(128)(4,1)} %bitcast.51), calls=%async_computation.7 | async-start | bytes 1048576
  101.4 2.8 %copy-start.15 = (bf16[512,3072]{1,0:T(8,128)(2,1)}, bf16[512,3072]{1,0:T(8,128)(2,1)S(1)}, u32[]{:S(2)}) copy-start(bf16[512,3072]{1,0:T(8,128)(2,1)S(1)} %get-tuple-element.72) | copy-start | bytes 9437188
  104.2 1.1 copy-start.3
  106.2 11.4 %slice-start = ((s8[4718592]{0:T(1024)(128)(4,1)}), s8[4194304]{0:T(1024)(128)(4,1)S(1)}, s32[]{:S(2)}) async-start(s8[4718592]{0:T(1024)(128)(4,1)} %bitcast.38), calls=%async_computation | async-start | bytes 8388608
  106.2 14.2 %slice-start.4 = ((s8[4718592]{0:T(1024)(128)(4,1)}), s8[4194304]{0:T(1024)(128)(4,1)S(1)}, s32[]{:S(2)}) async-start(s8[4718592]{0:T(1024)(128)(4,1)} %bitcast.49), calls=%async_computation.4 | async-start | bytes 8388608
  109.0 8.6 %slice-start.1 = ((s8[4718592]{0:T(1024)(128)(4,1)}), s8[524288]{0:T(1024)(128)(4,1)S(1)}, s32[]{:S(2)}) async-start(s8[4718592]{0:T(1024)(128)(4,1)} %bitcast.38), calls=%async_computation.1 | async-start | bytes 1048576
  109.0 11.3 %slice-start.5 = ((s8[4718592]{0:T(1024)(128)(4,1)}), s8[524288]{0:T(1024)(128)(4,1)S(1)}, s32[]{:S(2)}) async-start(s8[4718592]{0:T(1024)(128)(4,1)} %bitcast.49), calls=%async_computation.5 | async-start | bytes 1048576
  117.6 2.7 %copy-start.11 = (bf16[512,3072]{1,0:T(8,128)(2,1)}, bf16[512,3072]{1,0:T(8,128)(2,1)S(1)}, u32[]{:S(2)}) copy-start(bf16[512,3072]{1,0:T(8,128)(2,1)S(1)} %get-tuple-element.66) | copy-start | bytes 9437188
  117.6 2.7 %copy-start.13 = (bf16[512,3072]{1,0:T(8,128)(2,1)}, bf16[512,3072]{1,0:T(8,128)(2,1)S(1)}, u32[]{:S(2)}) copy-start(bf16[512,3072]{1,0:T(8,128)(2,1)S(1)} %get-tuple-element.65) | copy-start | bytes 9437188
  120.4 3.2 %copy-start.16 = (bf16[512,3072]{1,0:T(8,128)(2,1)S(1)}, bf16[512,3072]{1,0:T(8,128)(2,1)}, u32[]{:S(2)}) copy-start(bf16[512,3072]{1,0:T(8,128)(2,1)} %copy-done.15) | copy-start | bytes 9437188
  128.8 1.2 copy-start.6
  128.9 2.9 %copy-start.1 = (f32[512,768]{1,0:T(8,128)}, f32[512,768]{1,0:T(8,128)S(1)}, u32[]{:S(2)}) copy-start(f32[512,768]{1,0:T(8,128)S(1)} %broadcast_add_fusion.refs_16_) | copy-start | bytes 4718596
  130.0 4.9 %copy-start.14 = (bf16[512,3072]{1,0:T(8,128)(2,1)S(1)}, bf16[512,3072]{1,0:T(8,128)(2,1)}, u32[]{:S(2)}) copy-start(bf16[512,3072]{1,0:T(8,128)(2,1)} %copy-done.13) | copy-start | bytes 9437188
  131.8 3.0 %copy-start.5 = (bf16[512,768]{1,0:T(8,128)(2,1)S(1)}, bf16[512,768]{1,0:T(8,128)(2,1)}, u32[]{:S(2)}) copy-start(bf16[512,768]{1,0:T(8,128)(2,1)} %copy-done.4) | copy-start | bytes 2359300
  134.8 4.4 %copy-start.12 = (bf16[512,3072]{1,0:T(8,128)(2,1)S(1)}, bf16[512,3072]{1,0:T(8,128)(2,1)}, u32[]{:S(2)}) copy-start(bf16[512,3072]{1,0:T(8,128)(2,1)} %copy-done.11) | copy-start | bytes 9437188
  257.6 5.1 %copy-start.10 = (bf16[96,3072]{1,0:T(8,128)(2,1)S(1)}, bf16[96,3072]{1,0:T(8,128)(2,1)}, u32[]{:S(2)}) copy-start(bf16[96,3072]{1,0:T(8,128)(2,1)} %get-tuple-element.47) | copy-start | bytes 1769476
  260.6 3.2 %copy-start.9 = (bf16[96,3072]{1,0:T(8,128)(2,1)S(1)}, bf16[96,3072]{1,0:T(8,128)(2,1)}, u32[]{:S(2)}) copy-start(bf16[96,3072]{1,0:T(8,128)(2,1)} %get-tuple-element.48) | copy-start | bytes 1769476
  262.6 2.2 copy-start.8
  265.4 1.2 copy-start.7
where the time goes:
time: 268 us
  Pallas kernels  196 us (73%)
  matrix products  45.2 us (17%)
  other arithmetic  17.6 us (7%)
  local copies, waits for them, and re-layouts  7.39 us (3%)
    pallas_call x1, Pallas kernels, sum_grads(): pl.pallas_call(functools.partial(sum_kernel, plan), out_shape=[jax.ShapeD...  114 us
    pallas_call x1, Pallas kernels, gather_weights(): pl.pallas_call(functools.partial(gather_kernel, plan), out_shape=shapes +...  82.4 us
    dot_general x4, matrix products, transposed_product(): lax.dot_general(left, right, (((1,), (1,)), ((), ())), preferred_element_...  17.5 us
    dot_general x4, matrix products, token_contract(): lax.dot_general(left, right, (((0,), (0,)), ((), ())), preferred_element_...  15.1 us

commit v1 on v0

--- a/solution.py
+++ b/solution.py
@@ -18,6 +18,7 @@
 MESH = pl.DeviceIdType.MESH
 VMEM_LIMIT = 62 * 1024 * 1024
 SLACK = 2
+VMEM_MOST = 67043328
 AHEAD = 3
 
 
@@ -544,86 +545,95 @@
 
 
 def sum_kernel(plan, *refs):
-    mixing, gate, up, down, small = refs[:5]
-    carried, weight = refs[5:17], refs[17]
-    outs, small_out, input_grad = refs[18:22], refs[22], refs[23]
-    (held, mate_in, rep_in, z_in, final, small_in, load_sem, out_sem, small_sem, mate_send,
-     mate_recv, rep_send, rep_recv, z_send, z_recv, last_send, last_recv) = refs[24:41]
-    here, weight_here = refs[41:53], refs[53]
-    joined_low, joined, mask_bias, tokens_across, fetch_sem, result_sem = refs[54:60]
-    result_here = refs[60]
+    (gate_far, up_far, active_far, gate_weight, up_weight, down_weight, attention) = refs[:7]
+    carried = refs[7:23]
+    outs, small_out, input_grad = refs[23:27], refs[27], refs[28]
+    (pool, mate_in, rep_in, z_in, final, small_in, out_sem, small_sem, mate_send, mate_recv,
+     rep_send, rep_recv, z_send, z_recv, last_send, last_recv) = refs[29:45]
+    here = refs[45:61]
+    (weight, joined_low, mask_bias, across, branch, upper, small, gate_low, upward_low, active,
+     fetch_sem, tile_sem, weight_sem, result_sem) = refs[61:]
+    (query, key, value, attended, logsum, marks, segment_across, cosine, before, after, tokens,
+     inner_resid, grad, result_grad, normed_low, sums) = here
     rep, shard = lax.axis_index("rep"), lax.axis_index("shard")
     chips, piece, levels = plan.chips, plan.piece, plan.levels
     place, core = lax.div(shard, 2), lax.rem(shard, 2)
     mate = place * 2 + (1 - core)
-    rows = held.shape[2]
+    rows = pool.shape[2]
     total = plan.replicas * plan.shards
     early = 3 * chips
     count = 4 * chips
-    (query, key, value, upper, logsum, segment_down, segment_across, cosine, before, after, tokens,
-     inner_grad) = here
-    width = query.shape[1]
+    length, width = query.shape
     pairs = width // LANES
-
-    def fragments(turn, slab):
-        top = pl.multiple_of(slab * rows, 8)
-        if turn == 3:
-            wide = joined.shape[1]
-            return [
-                (joined.at[pl.ds(top, rows), :], 0, wide),
-                (mixing.at[pl.ds(top, rows), :], wide, mixing.shape[1]),
-            ]
-        if turn > 0:
-            return [((gate, up)[turn - 1].at[pl.ds(top, rows), :], 0, plan.width)]
-        wide = down.shape[1]
-        return [
-            (
-                down.at[
-                    pl.ds(pl.multiple_of(slab * (rows * (plan.width // wide)) + at * rows, 8), rows),
-                    :,
-                ],
-                at * wide,
-                wide,
-            )
-            for at in range(plan.width // wide)
-        ]
-
+    groups = plan.width // width
+    tile = width // 2
+    low_type, wide_type = jnp.bfloat16, jnp.float32
     gaps = list(range(1, chips)) + [0]
+    held = pool
 
     def slab_at(gap, which):
         return lax.rem(place + gap, chips) * 2 + which
 
-    def load(turn):
-        for gap in gaps:
-            for ref, left, wide in fragments(turn, slab_at(gap, core)):
-                pltpu.make_async_copy(
-                    ref, held.at[turn, gap, :, pl.ds(left, wide)], load_sem.at[turn, gap]
-                ).start()
-
-    def give(turn):
-        for gap in gaps:
-            for ref, left, wide in fragments(turn, slab_at(gap, 1 - core)):
-                remote(
-                    ref, mate_in.at[turn, gap, :, pl.ds(left, wide)],
-                    mate_send.at[turn, gap], mate_recv.at[turn, gap], rep, mate,
-                ).start()
-
-    for turn in range(3):
-        load(turn)
+    def stage(turn):
+        return 4 + turn % 3
+
+    def scatter(turn, slab, span, block):
+        gap = lax.rem(lax.div(slab, 2) - place + chips, chips)
+        other = lax.rem(slab + core, 2)
+        pool[turn + other * (stage(turn) - turn), gap, :, span] = block.astype(low_type)
+
+    def give(turn, gap):
+        remote(
+            pool.at[stage(turn), gap], mate_in.at[turn, gap],
+            mate_send.at[turn, gap], mate_recv.at[turn, gap], rep, mate,
+        ).start()
+
     fetches = [
         pltpu.make_async_copy(far, near, fetch_sem.at[at])
         for at, (far, near) in enumerate(zip(carried, here))
     ]
-    fetches.append(
-        pltpu.make_async_copy(
-            weight.at[:, pl.ds(0, 3 * width)], weight_here, fetch_sem.at[len(carried)]
+    late = fetches[:11]
+    soon = fetches[11:]
+    for fetch in soon + late:
+        fetch.start()
+
+    quarter = max(chips // groups, 1)
+    home = lax.rem(lax.div(place, quarter), groups)
+
+    def tile_start(at):
+        group = lax.rem(home + 1 + lax.div(at, 2), groups)
+        return group * width + lax.rem(at, 2) * tile
+
+    def slot_columns(left, slot):
+        return pl.ds(pl.multiple_of(left + slot * tile, LANES), tile)
+
+    def slot_rows(slot):
+        return pl.ds(pl.multiple_of(slot * tile, LANES), tile)
+
+    tail = pl.ds(4 * tile, width)
+
+    def tile_copies(at):
+        slot = lax.rem(at, 2)
+        span = pl.ds(pl.multiple_of(tile_start(at), LANES), tile)
+        pairs_of = (
+            (gate_far.at[:, span], gate_low.at[slot]),
+            (up_far.at[:, span], upward_low.at[slot]),
+            (active_far.at[:, span], active.at[slot]),
+            (gate_weight.at[:, span], weight.at[:, slot_columns(0, slot)]),
+            (up_weight.at[:, span], weight.at[:, slot_columns(2 * tile, slot)]),
+            (down_weight.at[span, :], weight.at[slot_rows(slot), tail]),
         )
-    )
-    for fetch in fetches:
-        fetch.start()
+        return [
+            pltpu.make_async_copy(far, near, tile_sem.at[number, slot])
+            for number, (far, near) in enumerate(pairs_of)
+        ]
+
+    for copy in tile_copies(0):
+        copy.start()
     greet_all(plan, rep, shard)
-    for turn in range(3):
-        give(turn)
+    for fetch in soon:
+        fetch.wait()
+    across[...] = normed_low[...].T
 
     def small_go(step, carry):
         other = lax.rem(rep * plan.shards + shard + step, total)
@@ -633,8 +643,6 @@
             other_rep, other_shard,
         ).start()
         return carry
-
-    lax.fori_loop(1, total, small_go, 0)
 
     def whole_mate(turn, gap):
         return remote(
@@ -674,9 +682,6 @@
     def advance(number, step):
         turn, gap = item_of(number)
         if step == 0:
-            pltpu.make_async_copy(
-                held.at[turn, gap], held.at[turn, gap], load_sem.at[turn, gap]
-            ).wait()
             whole_mate(turn, gap).wait_recv()
 
             def add(at, carry):
@@ -741,10 +746,10 @@
             for order in range(plan.orders):
                 span = pl.ds(plan.column(rep, order), piece)
                 part = pl.ds(order * piece, piece)
-                value = held[turn, 0, :, span].astype(jnp.float32)
+                amount = held[turn, 0, :, span].astype(jnp.float32)
                 for gap in range(1, chips):
-                    value = value + z_in[turn, gap - 1, :, part].astype(jnp.float32)
-                final[turn, :, span] = value.astype(jnp.bfloat16)
+                    amount = amount + z_in[turn, gap - 1, :, part].astype(jnp.float32)
+                final[turn, :, span] = amount.astype(jnp.bfloat16)
         else:
             for order in range(plan.orders):
                 await_spread(turn, order, step - 1)
@@ -755,11 +760,11 @@
 
     def tick(now):
         for step in reversed(range(levels + 1)):
-            late = now - (SLACK * (levels + step + 1) + chips - 1)
-
-            @pl.when((late >= 0) & (lax.rem(late + chips, chips) == 0) & (late < count))
-            def _(late=late, step=step):
-                finish(lax.div(late, chips), step)
+            behind = now - (SLACK * (levels + step + 1) + chips - 1)
+
+            @pl.when((behind >= 0) & (lax.rem(behind + chips, chips) == 0) & (behind < count))
+            def _(behind=behind, step=step):
+                finish(lax.div(behind, chips), step)
 
         for step in reversed(range(levels + 1)):
             number = now - SLACK * step
@@ -768,47 +773,186 @@
             def _(number=number, step=step):
                 advance(number, step)
 
-    tick(0)
-    for fetch in fetches:
+    block = min(length, 256)
+
+    def hidden(at, carry):
+        slot = lax.rem(at, 2)
+        for copy in tile_copies(at):
+            copy.wait()
+
+        @pl.when(at + 1 < 2 * groups)
+        def _():
+            for copy in tile_copies(at + 1):
+                copy.start()
+
+        start = tile_start(at)
+        span = pl.ds(pl.multiple_of(start, LANES), tile)
+        gate_tile = weight[:, slot_columns(0, slot)]
+        up_tile = weight[:, slot_columns(2 * tile, slot)]
+        down_tile = weight[slot_rows(slot), tail]
+
+        def some(number, carry):
+            some_rows = pl.ds(pl.multiple_of(number * block, block), block)
+            active_grad = product(result_grad[some_rows, :], down_tile, 1, 1)
+            gate = gate_low[slot, some_rows, :].astype(wide_type)
+            upward = upward_low[slot, some_rows, :].astype(wide_type)
+            sigmoid = 1.0 / (1.0 + jnp.exp(-gate))
+            gate_part = (
+                active_grad * upward * sigmoid * (1.0 + gate * (1.0 - sigmoid))
+            ).astype(low_type)
+            upward_part = (active_grad * (gate * sigmoid)).astype(low_type)
+            gate_low[slot, some_rows, :] = gate_part
+            upward_low[slot, some_rows, :] = upward_part
+            grad[some_rows, :] += product(gate_part, gate_tile, 1, 1) + product(
+                upward_part, up_tile, 1, 1
+            )
+            return carry
+
+        lax.fori_loop(0, length // block, some, 0)
+        down_part = product(active[slot], result_grad[...], 0, 0)
+        per = plan.width // width
+        for number in range(tile // rows):
+            chunk = lax.div(start, rows) + number
+            left = pl.multiple_of(lax.rem(chunk, per) * width, LANES)
+            scatter(
+                0, lax.div(chunk, per), pl.ds(left, width),
+                down_part[number * rows : (number + 1) * rows, :],
+            )
+        for turn, low in ((1, gate_low), (2, upward_low)):
+            for some_half in range(2):
+                top = some_half * (width // 2)
+                part = product(across[top : top + width // 2, :], low[slot], 1, 0)
+                for number in range(width // 2 // rows):
+                    scatter(
+                        turn, top // rows + number, span,
+                        part[number * rows : (number + 1) * rows, :],
+                    )
+        if chips == groups:
+            @pl.when(lax.rem(at, 2) == 1)
+            def _():
+                number = lax.div(at, 2)
+                give(0, lax.rem(number + 1, chips))
+
+                @pl.when(number > 0)
+                def _():
+                    tick(number - 1)
+        return carry
+
+    lax.fori_loop(0, 2 * groups, hidden, 0)
+    done = chips - 1 if chips == groups else 0
+    for gap in gaps:
+        if chips != groups:
+            give(0, gap)
+    for turn in (1, 2):
+        for gap in gaps:
+            give(turn, gap)
+    weight_load = pltpu.make_async_copy(attention, weight, weight_sem)
+    weight_load.start()
+    for fetch in late:
         fetch.wait()
-    mask_bias[...] = jnp.where(segment_down[:, 0:1] == segment_across[0:1, :], 0.0, NEG_LARGE)
-
-    def attend(now, carry):
-        @pl.when(now < pairs)
+    mask_bias[...] = jnp.where(marks[:, 0:1] == segment_across[0:1, :], 0.0, NEG_LARGE)
+
+    def norm_back():
+        gain = sums[4:5, :]
+        step_rows = min(length, 128)
+
+        def some(number, carry):
+            gain_sum, shift_sum = carry
+            some_rows = pl.ds(pl.multiple_of(number * step_rows, step_rows), step_rows)
+            centred = inner_resid[some_rows, :]
+            centred = centred - jnp.mean(centred, axis=1, keepdims=True)
+            inverse = lax.rsqrt(jnp.mean(centred * centred, axis=1, keepdims=True) + EPSILON)
+            normalized = centred * inverse
+            upstream = grad[some_rows, :]
+            gain_sum += jnp.sum(upstream * normalized, axis=0, keepdims=True)
+            shift_sum += jnp.sum(upstream, axis=0, keepdims=True)
+            scaled = upstream * gain
+            back = inverse * (
+                scaled
+                - jnp.mean(scaled, axis=1, keepdims=True)
+                - normalized * jnp.mean(scaled * normalized, axis=1, keepdims=True)
+            )
+            grad[some_rows, :] = back
+            branch[some_rows, :] = back.astype(low_type)
+            return gain_sum, shift_sum
+
+        nothing = jnp.zeros((1, width), wide_type)
+        gain_sum, shift_sum = lax.fori_loop(0, length // step_rows, some, (nothing, nothing))
+        sums[0:1, :] = gain_sum
+        sums[1:2, :] = shift_sum
+        vectors = sums[...]
+        for number in range(plan.shards):
+            small[number] = pltpu.roll(vectors, (width - rows * number) % width, 1)[:, :LANES]
+
+    def columns_loop(number, work):
+        def one(at, carry):
+            work(at)
+            return carry
+
+        lax.fori_loop(0, number, one, 0)
+
+    def raise_up():
+        weight_load.wait()
+
+        def one(at):
+            span = pl.ds(pl.multiple_of(at * 256, 256), 256)
+            upper[:, span] = product(
+                branch[...], weight[span, 3 * width : 4 * width], 1, 1
+            ).astype(low_type)
+
+        columns_loop(width // 256, one)
+
+    def weigh(left, right, lefts):
+        def one(at):
+            span = pl.ds(pl.multiple_of(left + at * tile, LANES), tile)
+            source = pl.ds(pl.multiple_of(at * tile, LANES), tile)
+            for some_half in range(2):
+                top = some_half * (width // 2)
+                part = product(across[top : top + width // 2, :], right[:, source], 1, 0)
+                for number in range(width // 2 // rows):
+                    scatter(
+                        3, top // rows + number, span, part[number * rows : (number + 1) * rows, :]
+                    )
+
+        columns_loop(lefts, one)
+
+    def middle(at, carry):
+        @pl.when(at == 0)
+        def _():
+            norm_back()
+            lax.fori_loop(1, total, small_go, 0)
+            raise_up()
+
+        @pl.when((at >= 1) & (at < pairs + 1))
         def _():
             back_pair(
-                now, query, key, value, upper, logsum, mask_bias, (cosine, before, after),
+                at - 1, query, key, value, upper, logsum, mask_bias, (cosine, before, after),
                 joined_low, width,
             )
 
-        @pl.when(now + 1 < early)
+        @pl.when(at + done < early)
         def _():
-            tick(now + 1)
+            tick(at + done)
         return carry
 
-    lax.fori_loop(0, max(pairs, early - 1), attend, 0)
-    tokens_across[...] = tokens[...].T
-
-    def weigh(at, carry):
-        span = pl.ds(pl.multiple_of(at * (width // 2), LANES), width // 2)
-        joined[:, span] = product(tokens_across[...], joined_low[:, span], 1, 0).astype(
-            jnp.bfloat16
-        )
-        return carry
-
-    lax.fori_loop(0, 6, weigh, 0)
-    load(3)
-    give(3)
-
-    def back(at, carry):
+    lax.fori_loop(0, max(pairs + 1, early - done), middle, 0)
+    for gap in gaps:
+        whole_mate(0, gap).wait_send()
+    across[...] = attended[...].T
+    weigh(3 * width, branch, width // tile)
+    across[...] = tokens[...].T
+    weigh(0, joined_low, 3 * width // tile)
+    for gap in gaps:
+        give(3, gap)
+
+    def back(at):
         low = pl.ds(pl.multiple_of(at * 256, 256), 256)
-        result_here[:, low] = (
-            inner_grad[:, low] + product(joined_low[...], weight_here[low, :], 1, 1)
+        result_grad[:, low] = (
+            grad[:, low] + product(joined_low[...], weight[low, 0 : 3 * width], 1, 1)
         ).astype(jnp.bfloat16)
-        return carry
-
-    lax.fori_loop(0, width // 256, back, 0)
-    result_copy = pltpu.make_async_copy(result_here, input_grad, result_sem)
+
+    columns_loop(width // 256, back)
+    result_copy = pltpu.make_async_copy(result_grad, input_grad, result_sem)
     result_copy.start()
 
     def late_tick(now, carry):
@@ -820,17 +964,20 @@
     everything = remote(small_in, small_in, small_sem.at[0], small_sem.at[1], rep, mate)
     everything.wait_recv()
 
-    def gain(at, value):
-        return value + small_in[at]
-
-    small_out[...] = lax.fori_loop(0, total - 1, gain, small[shard])
+    def gain_of(at, amount):
+        return amount + small_in[at]
+
+    small_out[...] = lax.fori_loop(0, total - 1, gain_of, small[shard])
     everything.wait_send()
     for turn in range(4):
         pltpu.make_async_copy(final.at[turn], outs[turn], out_sem.at[turn]).start()
 
     def drain(number, carry):
         turn, gap = item_of(number)
-        whole_mate(turn, gap).wait_send()
+
+        @pl.when(turn > 0)
+        def _():
+            whole_mate(turn, gap).wait_send()
         for order in range(plan.orders):
             for step in range(levels):
                 for copy in cross(turn, gap, order, step)[0]:
@@ -851,32 +998,31 @@
     result_copy.wait()
 
 
-def sum_grads(plan, grads, small, carried, weight):
+def sum_grads(plan, streamed, carried):
     hbm = pl.BlockSpec(memory_space=pl.ANY)
     vmem = pl.BlockSpec(memory_space=pltpu.VMEM)
     dma = pltpu.SemaphoreType.DMA
     chips, gaps, crossing = plan.chips, plan.chips - 1, plan.replicas - 1
-    rows = grads[0].shape[0] // plan.shards
-    low = jnp.bfloat16
+    length, width = carried[0].shape
+    rows = width // plan.shards
+    low, wide = jnp.bfloat16, jnp.float32
     total = plan.replicas * plan.shards
-    length, width = carried[0].shape
     return pl.pallas_call(
         functools.partial(sum_kernel, plan),
         out_shape=[jax.ShapeDtypeStruct((rows, plan.width), low)] * 4
         + [
-            jax.ShapeDtypeStruct(small.shape[1:], small.dtype),
+            jax.ShapeDtypeStruct((8, LANES), wide),
             jax.ShapeDtypeStruct((length, width), low),
         ],
-        in_specs=[hbm] * 4 + [vmem] + [hbm] * (len(carried) + 1),
+        in_specs=[hbm] * (len(streamed) + len(carried)),
         out_specs=[hbm] * 4 + [vmem, hbm],
         scratch_shapes=[
-            pltpu.VMEM((4, chips, rows, plan.width), low),
+            pltpu.VMEM((7, chips, rows, plan.width), low),
             pltpu.VMEM((4, chips, rows, plan.width), low),
             pltpu.VMEM((4, chips, plan.orders, crossing, rows, plan.piece), low),
             pltpu.VMEM((4, gaps, rows, plan.orders * plan.piece), low),
             pltpu.VMEM((4, rows, plan.width), low),
-            pltpu.VMEM((total - 1,) + small.shape[1:], small.dtype),
-            dma((4, chips)),
+            pltpu.VMEM((total - 1, 8, LANES), wide),
             dma((4,)),
             dma((2,)),
             dma((4, chips)),
@@ -890,38 +1036,32 @@
         ]
         + [pltpu.VMEM(array.shape, array.dtype) for array in carried]
         + [
-            pltpu.VMEM((width, 3 * width), low),
+            pltpu.VMEM((width, 4 * width), low),
             pltpu.VMEM((length, 3 * width), low),
-            pltpu.VMEM((width, 3 * width), low),
-            pltpu.VMEM((length, length), jnp.float32),
+            pltpu.VMEM((length, length), wide),
             pltpu.VMEM((width, length), low),
-            dma((len(carried) + 1,)),
+            pltpu.VMEM((length, width), low),
+            pltpu.VMEM((length, width), low),
+            pltpu.VMEM((plan.shards, 8, LANES), wide),
+            pltpu.VMEM((2, length, width // 2), low),
+            pltpu.VMEM((2, length, width // 2), low),
+            pltpu.VMEM((2, length, width // 2), low),
+            dma((len(carried),)),
+            dma((6, 2)),
             dma,
-            pltpu.VMEM((length, width), low),
+            dma,
         ],
         compiler_params=pltpu.CompilerParams(
-            collective_id=1, has_side_effects=True, vmem_limit_bytes=VMEM_LIMIT
+            collective_id=1, has_side_effects=True, vmem_limit_bytes=VMEM_MOST
         ),
         name="sum_grads",
-    )(*grads, small, *carried, weight)
+    )(*streamed, *carried)
 
 
 def layer_norm(values, gain, shift):
     centred = values - jnp.mean(values, axis=-1, keepdims=True)
     variance = jnp.mean(centred * centred, axis=-1, keepdims=True)
     return centred * lax.rsqrt(variance + EPSILON) * gain + shift
-
-
-def transposed_product(left, right):
-    return lax.dot_general(
-        left, right, (((1,), (1,)), ((), ())), preferred_element_type=jnp.float32
-    )
-
-
-def token_contract(left, right):
-    return lax.dot_general(
-        left, right, (((0,), (0,)), ((), ())), preferred_element_type=jnp.float32
-    )
 
 
 def on_device(
@@ -976,22 +1116,13 @@
         own_vectors,
         (tokens, marks, segments, jnp.asarray(np.tile(rates[None, :], (8, 1)))),
     )
-    mixing_full = attention_full[:, joined_weight.shape[1] :]
     vectors = vectors[:, :4, :part_rows].transpose(1, 0, 2).reshape(4, shards * part_rows)
     innergain_full, innershift_full, outergain_full, outershift_full = vectors
-    normed, inner_pull = jax.vjp(
-        layer_norm,
-        inner_resid,
-        innergain_full.astype(jnp.float32),
-        innershift_full.astype(jnp.float32),
-    )
+    normed = layer_norm(inner_resid, innergain_full, innershift_full)
     normed_low = normed.astype(jnp.bfloat16)
     gate_rows = jnp.dot(normed_low, gate_full, preferred_element_type=jnp.float32)
     upward = jnp.dot(normed_low, upward_full, preferred_element_type=jnp.float32)
-    active, silu_pull = jax.vjp(
-        lambda first, second: jax.nn.silu(first) * second, gate_rows, upward
-    )
-    active_low = active.astype(jnp.bfloat16)
+    active_low = (jax.nn.silu(gate_rows) * upward).astype(jnp.bfloat16)
     result = jnp.dot(active_low, down_full, preferred_element_type=jnp.float32)
     final, outer_pull = jax.vjp(
         layer_norm,
@@ -1000,40 +1131,29 @@
         outershift_full.astype(jnp.float32),
     )
     layer_output = final.astype(jnp.bfloat16)
-    gate_back, upward_back, down_back = gate_full, upward_full, down_full
     outer_grad, outergain_grad, outershift_grad = outer_pull(cotangent.astype(jnp.float32))
     result_grad = outer_grad.astype(jnp.bfloat16)
-    down_grad = token_contract(active_low, result_grad)
-    active_grad = transposed_product(result_grad, down_back)
-    gate_part, upward_part = silu_pull(active_grad)
-    gate_low = gate_part.astype(jnp.bfloat16)
-    upward_low = upward_part.astype(jnp.bfloat16)
-    gate_grad = token_contract(normed_low, gate_low)
-    up_grad = token_contract(normed_low, upward_low)
-    normed_grad = (
-        outer_grad
-        + transposed_product(gate_low, gate_back)
-        + transposed_product(upward_low, upward_back)
+    low = jnp.bfloat16
+    nothing = jnp.zeros_like(outergain_grad)
+    sums = jnp.stack(
+        [nothing, nothing, outergain_grad, outershift_grad, innergain_full] + [nothing] * 3
     )
-    inner_grad, innergain_grad, innershift_grad = inner_pull(normed_grad)
-    mixing_back = mixing_full
-    branch_grad = inner_grad.astype(jnp.bfloat16)
-    mixing_grad = token_contract(attended_low, branch_grad)
-    attended_grad = transposed_product(branch_grad, mixing_back).astype(jnp.bfloat16)
-
-    small = jnp.stack([innergain_grad, innershift_grad, outergain_grad, outershift_grad])
-    small = small.reshape(4, shards, part_rows).transpose(1, 0, 2)
-    small = jnp.pad(small, ((0, 0), (0, 4), (0, LANES - part_rows)))
-    low = jnp.bfloat16
     down_sum, gate_sum, up_sum, attention_sum, small_sum, input_grad = sum_grads(
         plan,
-        (mixing_grad.astype(low), gate_grad.astype(low), up_grad.astype(low), down_grad.astype(low)),
-        small,
+        (
+            gate_rows.astype(low),
+            upward.astype(low),
+            active_low,
+            gate_full,
+            upward_full,
+            down_full,
+            attention_full,
+        ),
         (
             query_low,
             key_low,
             value_low,
-            attended_grad,
+            attended_low,
             logsum,
             marks,
             segments,
@@ -1041,9 +1161,12 @@
             before,
             after,
             tokens,
-            inner_grad,
+            inner_resid,
+            outer_grad,
+            result_grad,
+            normed_low,
+            sums,
         ),
-        attention_full,
     )
     down_sum = down_sum.reshape(part_rows, -1, model_width).transpose(1, 0, 2)
     full = jnp.float32

time: 268 us -> 254 us (0.948)
  matrix products: 45.2 us -> 12.8 us
  Pallas kernels: 196 us -> 216 us
    dot_general x8 -> x0, matrix products: 32.6 us -> none  [the longest x4 17.5 us: transposed_product(): lax.dot_general(left, right, (((1,), (1,)), ((), ())), preferred_element_...]
    pallas_call x1, Pallas kernels: 114 us -> 134 us  [sum_grads(): pl.pallas_call(functools.partial(sum_kernel, plan), out_shape=[jax.ShapeD...]
    reduce_sum x3 -> x1, other arithmetic: 5.02 us -> 1.56 us  [layer_norm(): centred = values - jnp.mean(values, axis=-1, keepdims=True)]
where the time goes in v1:
time: 254 us; the launch traced here: 253 us
  Pallas kernels  216 us (85%)
  other arithmetic  18 us (7%)
  matrix products  12.8 us (5%)
  local copies, waits for them, and re-layouts  5.21 us (2%)
    pallas_call x1, Pallas kernels, sum_grads(): pl.pallas_call(functools.partial(sum_kernel, plan), out_shape=[jax.ShapeD...  134 us
    pallas_call x1, Pallas kernels, gather_weights(): pl.pallas_call(functools.partial(gather_kernel, plan), out_shape=shapes +...  82.4 us
    dot_general x1, matrix products, on_device(): jnp.dot(normed_low, upward_full, preferred_element_type=jnp.float32)  5.17 us

profile of v1, /device:TPU:0, one launch (start us, length us, event | category | flops | bytes accessed | tf_op | source)
XLA Modules:
  0.0 253.2 jit_solution(9978252767731583236)
XLA Ops:
  0.6 2.0 pad_maximum_fusion.refs_0_
  2.6 1.3 fusion.14.refs_4_
  3.9 1.6 broadcast_select_fusion.refs_6_.refs_12_
  5.5 82.4 %gather_weights.1 = (bf16[768,3072]{1,0:T(8,128)(2,1)}, bf16[768,3072]{1,0:T(8,128)(2,1)}, bf16[768,3072]{1,0:T(8,128)(2,1)}, bf16[3072,768]{1,0:T(8,128)(2,1)},...) custom-call(bf16[96,3072]{1,0:T(8,128)(2,1)} %pad_maximum_fusion.ref, ...), custom_call_target="tpu_custom_call" | custom-call | tf_op jit(solution)/shard_map/gather_weights/pallas_call | solution.py:466
  88.0 0.0 copy-start
  88.0 0.9 slice_bitcast_fusion
  88.8 0.1 slice_reduce_fusion.1
  88.9 0.1 add.48
  89.0 0.1 mul.89
  89.0 1.6 reduce_sum.70
  90.6 0.0 copy-done
  90.6 0.3 multiply_reduce_fusion.1
  90.9 0.0 slice-start
  90.9 0.3 fusion.4.refs_21_
  91.3 0.0 copy-start.2
  91.3 0.0 slice-start.1
  91.3 0.0 slice-start.2
  91.3 4.9 %fusion.23 = f32[512,3072]{1,0:T(8,128)S(1)} fusion(bf16[512,768]{1,0:T(8,128)(2,1)S(1)} %fusion.4.refs_21_, bf16[768,3072]{1,0:T(8,128)(2,1)} %get-tuple-element.33.refs_3_), kind=kOutput, calls=%fused_computation.56 | convolution fusion | flops 2415919104 | bytes 11796480 | tf_op jit(solution)/shard_map/dot_general | solution.py:1123
  96.2 0.0 copy-done.2
  96.2 0.0 slice-done
  96.3 0.0 slice-done.1
  96.3 0.0 slice-start.3
  96.3 5.2 %fusion.21 = (bf16[512,3072]{1,0:T(8,128)(2,1)}, bf16[512,3072]{1,0:T(8,128)(2,1)S(1)}, bf16[512,3072]{1,0:T(8,128)(2,1)}) fusion(f32[512,3072]{1,0:T(8,128)S(1)} %fusion.23, bf16[512,768]{1,0:T(8,128)(2,1)S(1)} %fusion.4.refs_21_, bf16[768,3072]{1,0:T(8,128)(2,1)S(1)} %bitcast.27), kind=kOutput, calls=%fused_computation.54 | convolution fusion | flops 2428502016 | bytes 21233664 | tf_op jit(solution)/shard_map/dot_general | solution.py:1124
  101.5 0.0 copy-start.3
  101.5 0.0 slice-done.2
  101.5 0.0 slice-done.3
  101.5 2.7 %fusion.22 = (f32[512]{0:T(512)S(1)}, f32[512,768]{1,0:T(8,128)S(1)}) fusion(bf16[512,3072]{1,0:T(8,128)(2,1)S(1)} %get-tuple-element.63.refs_2_, bf16[3072,768]{1,0:T(8,128)(2,1)S(1)} %bitcast.29, f32[768]{0:T(1024)S(1)} %add.48, f32[768]{0:T(1024)S(1)} %mul.89, f32[512]{0:T(512)S(1)} %add_rsqrt_fusion, f32[512,768]{1,0:T(8,128)S(1)} %copy-done, ...), kind=kOutput, calls=%fused_computation.55 | convolution fusion | flops 2418277888 | bytes 11022336 | tf_op jit(solution)/shard_map/dot_general | solution.py:1126
  104.2 0.0 copy-done.3
  104.2 0.0 copy-start.1
  104.2 0.1 mul.97
  104.3 1.8 fusion.2
  106.1 0.0 copy-done.1
  106.1 0.9 fusion.3
  107.0 0.1 add.54
  107.0 2.4 fusion.20
  109.4 0.1 unstack.18
  109.5 0.6 stack.25.refs_22_
  110.1 133.9 %sum_grads.1 = (bf16[96,3072]{1,0:T(8,128)(2,1)}, bf16[96,3072]{1,0:T(8,128)(2,1)}, bf16[96,3072]{1,0:T(8,128)(2,1)}, bf16[96,3072]{1,0:T(8,128)(2,1)}, f32[8,128]{1,0:T(8,128)}, /*index=5*/bf16[512,768]{1,0:T(8,128)(2,1)}) custom-call(bf16[512,3072]{1,0:T(8,128)(2,1)} %get-tuple-element.64.refs_0_, bf16[512,3072]{1,0:T(8,128)(2,1)} %get-tuple-element.62.refs_1_, ...), custom_call_target="tpu_custom_call" | custom-call | tf_op jit(solution)/shard_map/sum_grads/pallas_call | solution.py:1010
  244.0 0.0 copy-start.7
  244.0 0.0 copy-start.6
  244.0 2.1 slice_convert_fusion
  246.1 1.6 slice_convert_fusion.1
  247.8 0.0 copy-done.7
  247.8 0.0 copy-start.5
  247.8 1.1 convert_element_type.57
  248.9 0.0 copy-done.6
  248.9 1.1 convert_element_type.58
  250.0 0.0 copy-done.5
  250.0 0.6 reshape.93
  250.6 0.0 copy-start.8
  250.6 0.0 copy-start.4
  250.6 1.2 copy.25
  251.8 0.0 copy-done.8
  251.8 0.5 slice_bitcast_fusion.1
  252.3 0.0 copy-done.4
  252.3 0.9 copy.27
  (12 shorter events, 0.1 us)
Async XLA Ops:
  88.0 2.7 %copy-start = (f32[512,768]{1,0:T(8,128)S(1)}, f32[512,768]{1,0:T(8,128)}, u32[]{:S(2)}) copy-start(f32[512,768]{1,0:T(8,128)} %get-tuple-element.31.refs_18_) | copy-start | bytes 4718596
  90.9 5.3 %slice-start = ((s8[4718592]{0:T(1024)(128)(4,1)}), s8[4194304]{0:T(1024)(128)(4,1)S(1)}, s32[]{:S(2)}) async-start(s8[4718592]{0:T(1024)(128)(4,1)} %bitcast.26), calls=%async_computation | async-start | bytes 8388608
  91.3 5.0 %copy-start.2 = (bf16[512,768]{1,0:T(8,128)(2,1)}, bf16[512,768]{1,0:T(8,128)(2,1)S(1)}, u32[]{:S(2)}) copy-start(bf16[512,768]{1,0:T(8,128)(2,1)S(1)} %fusion.4.refs_21_) | copy-start | bytes 2359300
  91.3 5.0 %slice-start.1 = ((s8[4718592]{0:T(1024)(128)(4,1)}), s8[524288]{0:T(1024)(128)(4,1)S(1)}, s32[]{:S(2)}) async-start(s8[4718592]{0:T(1024)(128)(4,1)} %bitcast.26), calls=%async_computation.1 | async-start | bytes 1048576
  91.3 10.2 %slice-start.2 = ((s8[4718592]{0:T(1024)(128)(4,1)}), s8[4194304]{0:T(1024)(128)(4,1)S(1)}, s32[]{:S(2)}) async-start(s8[4718592]{0:T(1024)(128)(4,1)} %bitcast.28), calls=%async_computation.2 | async-start | bytes 8388608
  96.3 5.2 %slice-start.3 = ((s8[4718592]{0:T(1024)(128)(4,1)}), s8[524288]{0:T(1024)(128)(4,1)S(1)}, s32[]{:S(2)}) async-start(s8[4718592]{0:T(1024)(128)(4,1)} %bitcast.28), calls=%async_computation.3 | async-start | bytes 1048576
  101.5 2.7 %copy-start.3 = (bf16[512,3072]{1,0:T(8,128)(2,1)}, bf16[512,3072]{1,0:T(8,128)(2,1)S(1)}, u32[]{:S(2)}) copy-start(bf16[512,3072]{1,0:T(8,128)(2,1)S(1)} %get-tuple-element.63.refs_2_) | copy-start | bytes 9437188
  104.2 1.9 copy-start.1
  244.0 3.7 %copy-start.7 = (bf16[96,3072]{1,0:T(8,128)(2,1)S(1)}, bf16[96,3072]{1,0:T(8,128)(2,1)}, u32[]{:S(2)}) copy-start(bf16[96,3072]{1,0:T(8,128)(2,1)} %get-tuple-element.47) | copy-start | bytes 1769476
  244.0 4.9 %copy-start.6 = (bf16[96,3072]{1,0:T(8,128)(2,1)S(1)}, bf16[96,3072]{1,0:T(8,128)(2,1)}, u32[]{:S(2)}) copy-start(bf16[96,3072]{1,0:T(8,128)(2,1)} %get-tuple-element.48) | copy-start | bytes 1769476
  247.8 2.2 copy-start.5
  250.6 1.2 copy-start.8
  250.6 1.8 copy-start.4

commit v2 on v1

--- a/solution.py
+++ b/solution.py
@@ -140,16 +140,21 @@
 
 def gather_kernel(plan, *refs):
     own, small = refs[:4], refs[4]
-    carried = refs[5:9]
-    full, small_all = refs[9:13], refs[13]
-    results = refs[14:23]
-    stages = refs[23:27]
+    carried = refs[5:10]
+    full, small_all = refs[10:14], refs[14]
+    results = refs[15:34]
+    stages = refs[34:38]
     (load_sem, store_sem, small_send, small_recv, z_send, z_recv, rep_send, rep_recv, core_send,
-     core_recv) = refs[27:37]
-    tokens, marks, segment_across, rates = refs[37:41]
-    near = refs[41:50]
-    query, key, value, attended, logsum, inner_resid, cosine, before, after = near
-    weight, mask_bias, fetch_sem, weight_sem, result_sem = refs[50:55]
+     core_recv) = refs[38:48]
+    tokens, marks, segment_across, rates, cotangent = refs[48:53]
+    near = refs[53:72]
+    (query, key, value, attended, logsum, inner_resid, cosine, before, after, normed, normed_low,
+     vectors) = near[:12]
+    hidden_near, hidden_far = near[12:15], results[12:15]
+    gate_low, upward_low, active = hidden_near
+    outer_grad, result_grad, layer_output, sums = near[15:]
+    weight, mask_bias, fetch_sem, weight_sem, result_sem = refs[72:77]
+    hidden_weight, gate_rows, hidden_sem, down_near, down_sem, outer_sem = refs[77:]
     rep, shard = lax.axis_index("rep"), lax.axis_index("shard")
     chips, piece = plan.chips, plan.piece
     place, core = lax.div(shard, 2), lax.rem(shard, 2)
@@ -189,7 +194,7 @@
         load.start()
     fetches = [
         pltpu.make_async_copy(far, here, fetch_sem.at[at])
-        for at, (far, here) in enumerate(zip(carried, (tokens, marks, segment_across, rates)))
+        for at, (far, here) in enumerate(zip(carried, refs[48:53]))
     ]
     for fetch in fetches:
         fetch.start()
@@ -395,7 +400,7 @@
 
     copies = [
         pltpu.make_async_copy(here, far, result_sem.at[at])
-        for at, (here, far) in enumerate(zip(near, results))
+        for at, (here, far) in enumerate(zip(near[:12], results[:12]))
     ]
 
     def mix():
@@ -408,7 +413,137 @@
             return carry
 
         lax.fori_loop(0, width // 256, one, 0)
+
+    def normalize():
+        for step in range(1, plan.shards):
+            small_copy(step).wait_recv()
+        rest = jnp.zeros((8, width - LANES), jnp.float32)
+        whole = jnp.zeros((8, width), jnp.float32)
+        for number in range(plan.shards):
+            wide = jnp.concatenate([small_all[number], rest], axis=1)
+            whole = whole + pltpu.roll(wide, number * rows, 1)
+        vectors[...] = whole
+        step_rows = min(length, 128)
+
+        def some(at, carry):
+            some_rows = pl.ds(pl.multiple_of(at * step_rows, step_rows), step_rows)
+            centred = inner_resid[some_rows, :]
+            centred = centred - jnp.mean(centred, axis=1, keepdims=True)
+            inverse = lax.rsqrt(jnp.mean(centred * centred, axis=1, keepdims=True) + EPSILON)
+            amount = centred * inverse * vectors[0:1, :] + vectors[1:2, :]
+            normed[some_rows, :] = amount
+            normed_low[some_rows, :] = amount.astype(jnp.bfloat16)
+            return carry
+
+        lax.fori_loop(0, length // step_rows, some, 0)
         for copy in copies:
+            copy.start()
+
+    tiles = 2 * plan.width // width
+
+    def hidden_load(mat):
+        return pltpu.make_async_copy(full[mat], hidden_weight, weight_sem)
+
+    def hidden_copy(which, at):
+        span = pl.ds(pl.multiple_of(at * (width // 2), LANES), width // 2)
+        return pltpu.make_async_copy(
+            hidden_near[which].at[:, span], hidden_far[which].at[:, span], hidden_sem.at[which, at]
+        )
+
+    def fetch_hidden(mat):
+        await_core(mat)
+        hidden_load(mat).start()
+
+    def open_gate():
+        hidden_load(1).wait()
+
+        def one(at, carry):
+            span = pl.ds(pl.multiple_of(at * (width // 2), LANES), width // 2)
+            rows_of = product(normed_low[...], hidden_weight[:, span], 1, 0)
+            gate_rows[:, span] = rows_of
+            gate_low[:, span] = rows_of.astype(jnp.bfloat16)
+            hidden_copy(0, at).start()
+            return carry
+
+        lax.fori_loop(0, tiles, one, 0)
+
+    def activate():
+        hidden_load(2).wait()
+
+        def one(at, carry):
+            span = pl.ds(pl.multiple_of(at * (width // 2), LANES), width // 2)
+            upward = product(normed_low[...], hidden_weight[:, span], 1, 0)
+            gate = gate_rows[:, span]
+            upward_low[:, span] = upward.astype(jnp.bfloat16)
+            active[:, span] = (gate / (1.0 + jnp.exp(-gate)) * upward).astype(jnp.bfloat16)
+            hidden_copy(1, at).start()
+            hidden_copy(2, at).start()
+            return carry
+
+        lax.fori_loop(0, tiles, one, 0)
+
+    outer_copies = [
+        pltpu.make_async_copy(here, far, outer_sem.at[at])
+        for at, (here, far) in enumerate(zip(near[15:], results[15:]))
+    ]
+
+    def close():
+        depth = plan.width // width
+        loads = [
+            pltpu.make_async_copy(
+                full[3].at[pl.ds(at * width, width), :],
+                down_near.at[pl.ds(at * width, width), :],
+                down_sem.at[at],
+            )
+            for at in range(depth)
+        ]
+        for load in loads:
+            load.start()
+        block = min(length, 256)
+        for at in range(depth):
+            loads[at].wait()
+
+            def some(number, carry, at=at):
+                some_rows = pl.ds(pl.multiple_of(number * block, block), block)
+                base = normed if at == 0 else outer_grad
+                outer_grad[some_rows, :] = base[some_rows, :] + product(
+                    active[some_rows, at * width : (at + 1) * width],
+                    down_near[at * width : (at + 1) * width, :], 1, 0,
+                )
+                return carry
+
+            lax.fori_loop(0, length // block, some, 0)
+        gain, shift = vectors[2:3, :], vectors[3:4, :]
+        step_rows = min(length, 128)
+
+        def both(at, carry):
+            gain_sum, shift_sum = carry
+            some_rows = pl.ds(pl.multiple_of(at * step_rows, step_rows), step_rows)
+            centred = outer_grad[some_rows, :]
+            centred = centred - jnp.mean(centred, axis=1, keepdims=True)
+            inverse = lax.rsqrt(jnp.mean(centred * centred, axis=1, keepdims=True) + EPSILON)
+            normalized = centred * inverse
+            layer_output[some_rows, :] = (normalized * gain + shift).astype(jnp.bfloat16)
+            upstream = cotangent[some_rows, :].astype(jnp.float32)
+            gain_sum += jnp.sum(upstream * normalized, axis=0, keepdims=True)
+            shift_sum += jnp.sum(upstream, axis=0, keepdims=True)
+            scaled = upstream * gain
+            back = inverse * (
+                scaled
+                - jnp.mean(scaled, axis=1, keepdims=True)
+                - normalized * jnp.mean(scaled * normalized, axis=1, keepdims=True)
+            )
+            outer_grad[some_rows, :] = back
+            result_grad[some_rows, :] = back.astype(jnp.bfloat16)
+            return gain_sum, shift_sum
+
+        nothing = jnp.zeros((1, width), jnp.float32)
+        gain_sum, shift_sum = lax.fori_loop(0, length // step_rows, both, (nothing, nothing))
+        sums[...] = jnp.zeros_like(sums)
+        sums[2:3, :] = gain_sum
+        sums[3:4, :] = shift_sum
+        sums[4:5, :] = vectors[0:1, :]
+        for copy in outer_copies:
             copy.start()
 
     items = [(mat, number) for mat in range(4) for number in range(1, chips)]
@@ -424,15 +559,22 @@
         (2, functools.partial(attend, 0, pairs // 2)),
         (3, functools.partial(attend, pairs // 2, pairs)),
         (4, mix),
+        (4, normalize),
     ):
         events.append((ready + late, 1, work))
+    ahead = chips - 1
+    for due, work in (
+        (ready + ahead, functools.partial(fetch_hidden, 1)),
+        (max(ready + ahead, ready + 5), open_gate),
+        (max(ready + 2 * ahead, ready + 5), functools.partial(fetch_hidden, 2)),
+        (max(ready + 2 * ahead, ready + 5), activate),
+    ):
+        events.append((due, 2, work))
     for _, _, event in sorted(events, key=lambda event: event[:2]):
         event()
 
-    for mat in range(1, 4):
-        await_core(mat)
-    for step in range(1, plan.shards):
-        small_copy(step).wait_recv()
+    await_core(3)
+    close()
     for copy in sent:
         copy.wait_send()
     for mat in range(4):
@@ -440,6 +582,11 @@
         for number in range(1, chips):
             on(mat, number, lambda copy: copy.wait_send())
     for copy in copies:
+        copy.wait()
+    for which in range(3):
+        for at in range(tiles):
+            hidden_copy(which, at).wait()
+    for copy in outer_copies:
         copy.wait()
 
 
@@ -462,6 +609,18 @@
             jax.ShapeDtypeStruct((length, width), wide),
         ]
         + [jax.ShapeDtypeStruct((length, LANES), wide)] * 3
+        + [
+            jax.ShapeDtypeStruct((length, width), wide),
+            jax.ShapeDtypeStruct((length, width), low),
+            jax.ShapeDtypeStruct((8, width), wide),
+        ]
+        + [jax.ShapeDtypeStruct((length, plan.width), low)] * 3
+        + [
+            jax.ShapeDtypeStruct((length, width), wide),
+            jax.ShapeDtypeStruct((length, width), low),
+            jax.ShapeDtypeStruct((length, width), low),
+            jax.ShapeDtypeStruct((8, width), wide),
+        ]
     )
     return pl.pallas_call(
         functools.partial(gather_kernel, plan),
@@ -489,7 +648,13 @@
             pltpu.VMEM((length, length), wide),
             dma((len(carried),)),
             dma,
-            dma((len(results),)),
+            dma((12,)),
+            pltpu.VMEM(shapes[1].shape, low),
+            pltpu.VMEM((length, plan.width), wide),
+            dma((3, 2 * plan.width // width)),
+            pltpu.VMEM(shapes[3].shape, low),
+            dma((plan.width // width,)),
+            dma((4,)),
         ],
         compiler_params=pltpu.CompilerParams(
             collective_id=0, has_side_effects=True, vmem_limit_bytes=VMEM_LIMIT
@@ -1058,12 +1223,6 @@
     )(*streamed, *carried)
 
 
-def layer_norm(values, gain, shift):
-    centred = values - jnp.mean(values, axis=-1, keepdims=True)
-    variance = jnp.mean(centred * centred, axis=-1, keepdims=True)
-    return centred * lax.rsqrt(variance + EPSILON) * gain + shift
-
-
 def on_device(
     tokens,
     joined_weight,
@@ -1095,7 +1254,7 @@
         gate_full,
         upward_full,
         down_full,
-        vectors,
+        _,
         query_low,
         key_low,
         value_low,
@@ -1105,6 +1264,16 @@
         cosine_wide,
         before,
         after,
+        _,
+        normed_low,
+        _,
+        gate_low,
+        upward_low,
+        active_low,
+        outer_grad,
+        result_grad,
+        layer_output,
+        sums,
     ) = gather_weights(
         plan,
         (
@@ -1114,35 +1283,13 @@
             down_weight,
         ),
         own_vectors,
-        (tokens, marks, segments, jnp.asarray(np.tile(rates[None, :], (8, 1)))),
-    )
-    vectors = vectors[:, :4, :part_rows].transpose(1, 0, 2).reshape(4, shards * part_rows)
-    innergain_full, innershift_full, outergain_full, outershift_full = vectors
-    normed = layer_norm(inner_resid, innergain_full, innershift_full)
-    normed_low = normed.astype(jnp.bfloat16)
-    gate_rows = jnp.dot(normed_low, gate_full, preferred_element_type=jnp.float32)
-    upward = jnp.dot(normed_low, upward_full, preferred_element_type=jnp.float32)
-    active_low = (jax.nn.silu(gate_rows) * upward).astype(jnp.bfloat16)
-    result = jnp.dot(active_low, down_full, preferred_element_type=jnp.float32)
-    final, outer_pull = jax.vjp(
-        layer_norm,
-        normed + result,
-        outergain_full.astype(jnp.float32),
-        outershift_full.astype(jnp.float32),
-    )
-    layer_output = final.astype(jnp.bfloat16)
-    outer_grad, outergain_grad, outershift_grad = outer_pull(cotangent.astype(jnp.float32))
-    result_grad = outer_grad.astype(jnp.bfloat16)
-    low = jnp.bfloat16
-    nothing = jnp.zeros_like(outergain_grad)
-    sums = jnp.stack(
-        [nothing, nothing, outergain_grad, outershift_grad, innergain_full] + [nothing] * 3
+        (tokens, marks, segments, jnp.asarray(np.tile(rates[None, :], (8, 1))), cotangent),
     )
     down_sum, gate_sum, up_sum, attention_sum, small_sum, input_grad = sum_grads(
         plan,
         (
-            gate_rows.astype(low),
-            upward.astype(low),
+            gate_low,
+            upward_low,
             active_low,
             gate_full,
             upward_full,

time: 254 us -> 245 us (0.965)
  matrix products: 12.8 us -> 0 us
  Pallas kernels: 216 us -> 228 us
  other arithmetic: 18 us -> 10.8 us
    dot_general x3 -> x0, matrix products: 12.8 us -> none  [the longest x1 5.17 us: on_device(): jnp.dot(normed_low, upward_full, preferred_element_type=jnp.float32)]
    pallas_call x1, Pallas kernels: 82.4 us -> 91.8 us  [gather_weights(): pl.pallas_call(functools.partial(gather_kernel, plan), out_shape=shapes +...]
    reduce_sum x4 -> x0, other arithmetic: 4.52 us -> none  [the longest x2 2.66 us: layer_norm(): return centred * lax.rsqrt(variance + EPSILON) * gain + shift]
    pallas_call x1, Pallas kernels: 134 us -> 137 us  [sum_grads(): pl.pallas_call(functools.partial(sum_kernel, plan), out_shape=[jax.ShapeD...]
    convert_element_type x2 -> x0, other arithmetic: 2.66 us -> none  [the longest x1 2.35 us: on_device(): result_grad = outer_grad.astype(jnp.bfloat16)]
where the time goes in v2:
time: 245 us
  Pallas kernels  228 us (93%)
  other arithmetic  10.8 us (4%)
  local copies, waits for them, and re-layouts  4.92 us (2%)
    pallas_call x1, Pallas kernels, sum_grads(): pl.pallas_call(functools.partial(sum_kernel, plan), out_shape=[jax.ShapeD...  137 us
    pallas_call x1, Pallas kernels, gather_weights(): pl.pallas_call(functools.partial(gather_kernel, plan), out_shape=shapes +...  91.8 us

profile of v2, /device:TPU:0, one launch (start us, length us, event | category | flops | bytes accessed | tf_op | source)
XLA Modules:
  0.0 244.8 jit_solution(12042867890075319989)
XLA Ops:
  0.7 1.3 fusion.9.refs_4_
  2.0 1.6 broadcast_select_fusion.refs_6_.refs_12_
  3.6 2.0 pad_maximum_fusion.refs_0_
  5.5 91.8 %gather_weights.1 = (bf16[768,3072]{1,0:T(8,128)(2,1)}, bf16[768,3072]{1,0:T(8,128)(2,1)}, bf16[768,3072]{1,0:T(8,128)(2,1)}, bf16[3072,768]{1,0:T(8,128)(2,1)},...) custom-call(bf16[96,3072]{1,0:T(8,128)(2,1)} %pad_maximum_fusion.ref, ...), custom_call_target="tpu_custom_call" | custom-call | tf_op jit(solution)/shard_map/gather_weights/pallas_call | solution.py:625
  97.4 136.6 %sum_grads.1 = (bf16[96,3072]{1,0:T(8,128)(2,1)}, bf16[96,3072]{1,0:T(8,128)(2,1)}, bf16[96,3072]{1,0:T(8,128)(2,1)}, bf16[96,3072]{1,0:T(8,128)(2,1)}, f32[8,128]{1,0:T(8,128)}, /*index=5*/bf16[512,768]{1,0:T(8,128)(2,1)}) custom-call(bf16[512,3072]{1,0:T(8,128)(2,1)} %get-tuple-element.39.refs_0_, bf16[512,3072]{1,0:T(8,128)(2,1)} %get-tuple-element.40.refs_1_, ...), custom_call_target="tpu_custom_call" | custom-call | tf_op jit(solution)/shard_map/sum_grads/pallas_call | solution.py:1175
  233.9 0.0 copy-start.4
  234.0 1.4 slice_bitcast_fusion
  235.3 1.6 slice_convert_fusion.1
  237.0 0.0 copy-start.3
  237.0 2.0 slice_convert_fusion
  239.0 0.0 copy-done.4
  239.0 0.0 copy-start.2
  239.0 1.1 convert_element_type.29
  240.1 0.0 copy-done.3
  240.1 1.1 convert_element_type.30
  241.2 0.0 copy-done.2
  241.2 0.6 reshape.36
  241.8 0.0 copy-start
  241.8 0.0 copy-start.1
  241.8 1.2 copy.25
  243.1 0.0 copy-done
  243.1 0.9 copy.28
  243.9 0.0 copy-done.1
  243.9 0.9 copy.29
  (1 shorter events, 0.0 us)
Async XLA Ops:
  233.9 5.1 %copy-start.4 = (bf16[96,3072]{1,0:T(8,128)(2,1)S(1)}, bf16[96,3072]{1,0:T(8,128)(2,1)}, u32[]{:S(2)}) copy-start(bf16[96,3072]{1,0:T(8,128)(2,1)} %get-tuple-element.61) | copy-start | bytes 1769476
  237.0 3.2 %copy-start.3 = (bf16[96,3072]{1,0:T(8,128)(2,1)S(1)}, bf16[96,3072]{1,0:T(8,128)(2,1)}, u32[]{:S(2)}) copy-start(bf16[96,3072]{1,0:T(8,128)(2,1)} %get-tuple-element.62) | copy-start | bytes 1769476
  239.0 2.2 copy-start.2
  241.8 1.2 copy-start
  241.8 2.1 copy-start.1

commit v3 on v2

--- a/solution.py
+++ b/solution.py
@@ -19,6 +19,7 @@
 VMEM_LIMIT = 62 * 1024 * 1024
 SLACK = 2
 VMEM_MOST = 67043328
+LIFTS = 2
 AHEAD = 3
 
 
@@ -716,8 +717,8 @@
     (pool, mate_in, rep_in, z_in, final, small_in, out_sem, small_sem, mate_send, mate_recv,
      rep_send, rep_recv, z_send, z_recv, last_send, last_recv) = refs[29:45]
     here = refs[45:61]
-    (weight, joined_low, mask_bias, across, branch, upper, small, gate_low, upward_low, active,
-     fetch_sem, tile_sem, weight_sem, result_sem) = refs[61:]
+    (weight, gate_low, mask_bias, across, branch, upper, small, upward_low, active, fetch_sem,
+     tile_sem, weight_sem, result_sem) = refs[61:]
     (query, key, value, attended, logsum, marks, segment_across, cosine, before, after, tokens,
      inner_resid, grad, result_grad, normed_low, sums) = here
     rep, shard = lax.axis_index("rep"), lax.axis_index("shard")
@@ -735,6 +736,7 @@
     low_type, wide_type = jnp.bfloat16, jnp.float32
     gaps = list(range(1, chips)) + [0]
     held = pool
+    joined_low = gate_low
 
     def slab_at(gap, which):
         return lax.rem(place + gap, chips) * 2 + which
@@ -781,15 +783,25 @@
         slot = lax.rem(at, 2)
         span = pl.ds(pl.multiple_of(tile_start(at), LANES), tile)
         pairs_of = (
-            (gate_far.at[:, span], gate_low.at[slot]),
-            (up_far.at[:, span], upward_low.at[slot]),
+            (gate_far.at[:, span], gate_low.at[:, span]),
+            (up_far.at[:, span], upward_low.at[:, span]),
             (active_far.at[:, span], active.at[slot]),
-            (gate_weight.at[:, span], weight.at[:, slot_columns(0, slot)]),
-            (up_weight.at[:, span], weight.at[:, slot_columns(2 * tile, slot)]),
             (down_weight.at[span, :], weight.at[slot_rows(slot), tail]),
         )
         return [
             pltpu.make_async_copy(far, near, tile_sem.at[number, slot])
+            for number, (far, near) in enumerate(pairs_of)
+        ]
+
+    def lift_copies(at):
+        slot = lax.rem(at, 2)
+        span = pl.ds(pl.multiple_of(at * tile, LANES), tile)
+        pairs_of = (
+            (gate_weight.at[:, span], weight.at[:, slot_columns(0, slot)]),
+            (up_weight.at[:, span], weight.at[:, slot_columns(2 * tile, slot)]),
+        )
+        return [
+            pltpu.make_async_copy(far, near, tile_sem.at[4 + number, slot])
             for number, (far, near) in enumerate(pairs_of)
         ]
 
@@ -952,25 +964,18 @@
 
         start = tile_start(at)
         span = pl.ds(pl.multiple_of(start, LANES), tile)
-        gate_tile = weight[:, slot_columns(0, slot)]
-        up_tile = weight[:, slot_columns(2 * tile, slot)]
         down_tile = weight[slot_rows(slot), tail]
 
         def some(number, carry):
             some_rows = pl.ds(pl.multiple_of(number * block, block), block)
             active_grad = product(result_grad[some_rows, :], down_tile, 1, 1)
-            gate = gate_low[slot, some_rows, :].astype(wide_type)
-            upward = upward_low[slot, some_rows, :].astype(wide_type)
+            gate = gate_low[some_rows, span].astype(wide_type)
+            upward = upward_low[some_rows, span].astype(wide_type)
             sigmoid = 1.0 / (1.0 + jnp.exp(-gate))
-            gate_part = (
+            gate_low[some_rows, span] = (
                 active_grad * upward * sigmoid * (1.0 + gate * (1.0 - sigmoid))
             ).astype(low_type)
-            upward_part = (active_grad * (gate * sigmoid)).astype(low_type)
-            gate_low[slot, some_rows, :] = gate_part
-            upward_low[slot, some_rows, :] = upward_part
-            grad[some_rows, :] += product(gate_part, gate_tile, 1, 1) + product(
-                upward_part, up_tile, 1, 1
-            )
+            upward_low[some_rows, span] = (active_grad * (gate * sigmoid)).astype(low_type)
             return carry
 
         lax.fori_loop(0, length // block, some, 0)
@@ -986,7 +991,7 @@
         for turn, low in ((1, gate_low), (2, upward_low)):
             for some_half in range(2):
                 top = some_half * (width // 2)
-                part = product(across[top : top + width // 2, :], low[slot], 1, 0)
+                part = product(across[top : top + width // 2, :], low[:, span], 1, 0)
                 for number in range(width // 2 // rows):
                     scatter(
                         turn, top // rows + number, span,
@@ -1005,6 +1010,8 @@
 
     lax.fori_loop(0, 2 * groups, hidden, 0)
     done = chips - 1 if chips == groups else 0
+    for copy in lift_copies(0):
+        copy.start()
     for gap in gaps:
         if chips != groups:
             give(0, gap)
@@ -1012,10 +1019,32 @@
         for gap in gaps:
             give(turn, gap)
     weight_load = pltpu.make_async_copy(attention, weight, weight_sem)
-    weight_load.start()
     for fetch in late:
         fetch.wait()
     mask_bias[...] = jnp.where(marks[:, 0:1] == segment_across[0:1, :], 0.0, NEG_LARGE)
+
+    def lift(at, carry):
+        slot = lax.rem(at, 2)
+        for copy in lift_copies(at):
+            copy.wait()
+
+        @pl.when(at + 1 < 2 * groups)
+        def _():
+            for copy in lift_copies(at + 1):
+                copy.start()
+
+        span = pl.ds(pl.multiple_of(at * tile, LANES), tile)
+
+        def some(number, carry):
+            some_rows = pl.ds(pl.multiple_of(number * block, block), block)
+            grad[some_rows, :] += product(
+                gate_low[some_rows, span], weight[:, slot_columns(0, slot)], 1, 1
+            ) + product(
+                upward_low[some_rows, span], weight[:, slot_columns(2 * tile, slot)], 1, 1
+            )
+            return carry
+
+        return lax.fori_loop(0, length // block, some, carry)
 
     def norm_back():
         gain = sums[4:5, :]
@@ -1082,16 +1111,21 @@
         columns_loop(lefts, one)
 
     def middle(at, carry):
-        @pl.when(at == 0)
+        @pl.when(at < LIFTS)
         def _():
+            lax.fori_loop(at * 2 * groups // LIFTS, (at + 1) * 2 * groups // LIFTS, lift, 0)
+
+        @pl.when(at == LIFTS)
+        def _():
+            weight_load.start()
             norm_back()
             lax.fori_loop(1, total, small_go, 0)
             raise_up()
 
-        @pl.when((at >= 1) & (at < pairs + 1))
+        @pl.when((at > LIFTS) & (at < LIFTS + 1 + pairs))
         def _():
             back_pair(
-                at - 1, query, key, value, upper, logsum, mask_bias, (cosine, before, after),
+                at - LIFTS - 1, query, key, value, upper, logsum, mask_bias, (cosine, before, after),
                 joined_low, width,
             )
 
@@ -1100,7 +1134,7 @@
             tick(at + done)
         return carry
 
-    lax.fori_loop(0, max(pairs + 1, early - done), middle, 0)
+    lax.fori_loop(0, max(LIFTS + 1 + pairs, early - done), middle, 0)
     for gap in gaps:
         whole_mate(0, gap).wait_send()
     across[...] = attended[...].T
@@ -1113,7 +1147,7 @@
     def back(at):
         low = pl.ds(pl.multiple_of(at * 256, 256), 256)
         result_grad[:, low] = (
-            grad[:, low] + product(joined_low[...], weight[low, 0 : 3 * width], 1, 1)
+            grad[:, low] + product(joined_low[:, 0 : 3 * width], weight[low, 0 : 3 * width], 1, 1)
         ).astype(jnp.bfloat16)
 
     columns_loop(width // 256, back)
@@ -1202,14 +1236,13 @@
         + [pltpu.VMEM(array.shape, array.dtype) for array in carried]
         + [
             pltpu.VMEM((width, 4 * width), low),
-            pltpu.VMEM((length, 3 * width), low),
+            pltpu.VMEM((length, plan.width), low),
             pltpu.VMEM((length, length), wide),
             pltpu.VMEM((width, length), low),
             pltpu.VMEM((length, width), low),
             pltpu.VMEM((length, width), low),
             pltpu.VMEM((plan.shards, 8, LANES), wide),
-            pltpu.VMEM((2, length, width // 2), low),
-            pltpu.VMEM((2, length, width // 2), low),
+            pltpu.VMEM((length, plan.width), low),
             pltpu.VMEM((2, length, width // 2), low),
             dma((len(carried),)),
             dma((6, 2)),

time: 245 us -> 239 us (0.976)
  Pallas kernels: 228 us -> 222 us
    pallas_call x1, Pallas kernels: 137 us -> 130 us  [sum_grads(): pl.pallas_call(functools.partial(sum_kernel, plan), out_shape=[jax.ShapeD...]
where the time goes in v3:
time: 239 us; the launch traced here: 238 us
  Pallas kernels  222 us (93%)
  other arithmetic  10.8 us (5%)
  local copies, waits for them, and re-layouts  4.92 us (2%)
    pallas_call x1, Pallas kernels, sum_grads(): pl.pallas_call(functools.partial(sum_kernel, plan), out_shape=[jax.ShapeD...  130 us
    pallas_call x1, Pallas kernels, gather_weights(): pl.pallas_call(functools.partial(gather_kernel, plan), out_shape=shapes +...  91.8 us

profile of v3, /device:TPU:0, one launch (start us, length us, event | category | flops | bytes accessed | tf_op | source)
XLA Modules:
  0.0 238.3 jit_solution(7133344703061715622)
XLA Ops:
  0.7 1.3 fusion.9.refs_4_
  2.0 1.6 broadcast_select_fusion.refs_6_.refs_12_
  3.6 2.0 pad_maximum_fusion.refs_0_
  5.5 91.8 %gather_weights.1 = (bf16[768,3072]{1,0:T(8,128)(2,1)}, bf16[768,3072]{1,0:T(8,128)(2,1)}, bf16[768,3072]{1,0:T(8,128)(2,1)}, bf16[3072,768]{1,0:T(8,128)(2,1)},...) custom-call(bf16[96,3072]{1,0:T(8,128)(2,1)} %pad_maximum_fusion.ref, ...), custom_call_target="tpu_custom_call" | custom-call | tf_op jit(solution)/shard_map/gather_weights/pallas_call | solution.py:626
  97.4 130.1 %sum_grads.1 = (bf16[96,3072]{1,0:T(8,128)(2,1)}, bf16[96,3072]{1,0:T(8,128)(2,1)}, bf16[96,3072]{1,0:T(8,128)(2,1)}, bf16[96,3072]{1,0:T(8,128)(2,1)}, f32[8,128]{1,0:T(8,128)}, /*index=5*/bf16[512,768]{1,0:T(8,128)(2,1)}) custom-call(bf16[512,3072]{1,0:T(8,128)(2,1)} %get-tuple-element.39.refs_0_, bf16[512,3072]{1,0:T(8,128)(2,1)} %get-tuple-element.40.refs_1_, ...), custom_call_target="tpu_custom_call" | custom-call | tf_op jit(solution)/shard_map/sum_grads/pallas_call | solution.py:1209
  227.5 0.0 copy-start.4
  227.5 1.4 slice_bitcast_fusion
  228.8 1.6 slice_convert_fusion.1
  230.5 0.0 copy-start.3
  230.5 2.0 slice_convert_fusion
  232.5 0.0 copy-done.4
  232.5 0.0 copy-start.2
  232.5 1.1 convert_element_type.29
  233.6 0.0 copy-done.3
  233.6 1.1 convert_element_type.30
  234.7 0.0 copy-done.2
  234.7 0.6 reshape.36
  235.3 0.0 copy-start
  235.3 0.0 copy-start.1
  235.3 1.2 copy.25
  236.6 0.0 copy-done
  236.6 0.9 copy.28
  237.4 0.0 copy-done.1
  237.4 0.9 copy.29
  (1 shorter events, 0.0 us)
Async XLA Ops:
  227.5 5.1 %copy-start.4 = (bf16[96,3072]{1,0:T(8,128)(2,1)S(1)}, bf16[96,3072]{1,0:T(8,128)(2,1)}, u32[]{:S(2)}) copy-start(bf16[96,3072]{1,0:T(8,128)(2,1)} %get-tuple-element.61) | copy-start | bytes 1769476
  230.5 3.2 %copy-start.3 = (bf16[96,3072]{1,0:T(8,128)(2,1)S(1)}, bf16[96,3072]{1,0:T(8,128)(2,1)}, u32[]{:S(2)}) copy-start(bf16[96,3072]{1,0:T(8,128)(2,1)} %get-tuple-element.62) | copy-start | bytes 1769476
  232.5 2.2 copy-start.2
  235.3 1.2 copy-start
  235.3 2.1 copy-start.1

commit v4 on v3

--- a/solution.py
+++ b/solution.py
@@ -139,7 +139,7 @@
         attended[at * block : (at + 1) * block, span] = part.astype(jnp.bfloat16)
 
 
-def gather_kernel(plan, *refs):
+def gather_kernel(plan, mixing_own, *refs):
     own, small = refs[:4], refs[4]
     carried = refs[5:10]
     full, small_all = refs[10:14], refs[14]
@@ -190,7 +190,17 @@
         copy.start()
         sent.append(copy)
 
-    loads = [pltpu.make_async_copy(own[mat], stages[mat], load_sem.at[mat]) for mat in range(4)]
+    mine = (stages[0],) + tuple(own[1:])
+    joined_own = own[0].shape[1]
+    loads = [
+        pltpu.make_async_copy(own[0], stages[0].at[:, pl.ds(0, joined_own)], load_sem.at[0])
+    ]
+    loads += [pltpu.make_async_copy(own[mat], stages[mat], load_sem.at[mat]) for mat in range(1, 4)]
+    loads.append(
+        pltpu.make_async_copy(
+            mixing_own, stages[0].at[:, pl.ds(joined_own, mixing_own.shape[1])], load_sem.at[4]
+        )
+    )
     for load in loads:
         load.start()
     fetches = [
@@ -227,7 +237,7 @@
         )
 
     def own_hop(mat, down, order):
-        return hop(mat, place, down, order, part(own[mat], mat, 0, rep, order))
+        return hop(mat, place, down, order, part(mine[mat], mat, 0, rep, order))
 
     def next_hop(mat, number, order):
         origin, above = nearest(number)
@@ -257,11 +267,12 @@
 
     def give(mat):
         launch(remote(
-            own[mat], slab_of(mat, shard), core_send.at[mat, 0], core_recv.at[mat, 0], rep, mate
+            mine[mat], slab_of(mat, shard), core_send.at[mat, 0], core_recv.at[mat, 0], rep, mate
         ))
 
-    for mat in range(2):
-        along(mat, lambda copy: copy.start())
+    for load in (loads[0], loads[4]):
+        load.wait()
+    along(0, lambda copy: copy.start())
     give(0)
     for step in range(1, plan.shards):
         launch(small_copy(step))
@@ -269,7 +280,8 @@
         give(mat)
     stores = []
     for mat in range(4):
-        loads[mat].wait()
+        if mat > 0:
+            loads[mat].wait()
         store = pltpu.make_async_copy(stages[mat], slab_of(mat, shard), store_sem.at[mat])
         store.start()
         stores.append(store)
@@ -331,8 +343,8 @@
                     launch(copy)
         if step == 0:
             on(mat, number, lambda copy: copy.start())
-            if number == 1 and mat + 2 < 4:
-                along(mat + 2, lambda copy: copy.start())
+            if number == 1 and mat + 1 < 4:
+                along(mat + 1, lambda copy: copy.start())
         if step == plan.levels:
             there = slab_of(mat, source(number))
             launch(remote(
@@ -595,9 +607,12 @@
     hbm = pl.BlockSpec(memory_space=pl.ANY)
     vmem = pl.BlockSpec(memory_space=pltpu.VMEM)
     dma = pltpu.SemaphoreType.DMA
+    pieces = [jax.ShapeDtypeStruct((own[1].shape[0], plan.width), own[1].dtype)] + [
+        jax.ShapeDtypeStruct(array.shape, array.dtype) for array in own[2:]
+    ]
     shapes = [
         jax.ShapeDtypeStruct((array.shape[0] * plan.shards, array.shape[1]), array.dtype)
-        for array in own
+        for array in pieces
     ]
     gaps = plan.chips - 1
     crossing = plan.replicas - 1
@@ -627,11 +642,11 @@
         functools.partial(gather_kernel, plan),
         out_shape=shapes + [jax.ShapeDtypeStruct((plan.shards,) + small.shape, small.dtype)]
         + results,
-        in_specs=[hbm] * 4 + [vmem] + [hbm] * len(carried),
+        in_specs=[hbm] * 5 + [vmem] + [hbm] * len(carried),
         out_specs=[hbm] * 4 + [vmem] + [hbm] * len(results),
-        scratch_shapes=[pltpu.VMEM(array.shape, array.dtype) for array in own]
+        scratch_shapes=[pltpu.VMEM(array.shape, array.dtype) for array in pieces]
         + [
-            dma((4,)),
+            dma((5,)),
             dma((4,)),
             dma((plan.shards - 1,)),
             dma((plan.shards - 1,)),
@@ -1310,7 +1325,8 @@
     ) = gather_weights(
         plan,
         (
-            jnp.concatenate([joined_weight, mixing_weight], axis=1),
+            mixing_weight,
+            joined_weight,
             gate_weight,
             up_weight,
             down_weight,

time: 239 us -> 235 us (0.983)
  Pallas kernels: 222 us -> 219 us
where the time goes in v4:
time: 235 us; the launch traced here: 234 us
  Pallas kernels  219 us (93%)
  other arithmetic  9.83 us (4%)
  local copies, waits for them, and re-layouts  4.91 us (2%)
    pallas_call x1, Pallas kernels, sum_grads(): pl.pallas_call(functools.partial(sum_kernel, plan), out_shape=[jax.ShapeD...  129 us
    pallas_call x1, Pallas kernels, gather_weights(): pl.pallas_call(functools.partial(gather_kernel, plan), out_shape=shapes +...  89.9 us

profile of v4, /device:TPU:0, one launch (start us, length us, event | category | flops | bytes accessed | tf_op | source)
XLA Modules:
  0.0 234.4 jit_solution(15694381649083022512)
XLA Ops:
  0.7 1.3 fusion.9.refs_4_
  2.0 1.6 broadcast_select_fusion.refs_6_.refs_12_
  3.6 89.9 %gather_weights.1 = (bf16[768,3072]{1,0:T(8,128)(2,1)}, bf16[768,3072]{1,0:T(8,128)(2,1)}, bf16[768,3072]{1,0:T(8,128)(2,1)}, bf16[3072,768]{1,0:T(8,128)(2,1)},...) custom-call(bf16[96,768]{1,0:T(8,128)(2,1)} %mixing_own.1, ...), custom_call_target="tpu_custom_call" | custom-call | tf_op jit(solution)/shard_map/gather_weights/pallas_call | solution.py:641
  93.5 129.0 %sum_grads.1 = (bf16[96,3072]{1,0:T(8,128)(2,1)}, bf16[96,3072]{1,0:T(8,128)(2,1)}, bf16[96,3072]{1,0:T(8,128)(2,1)}, bf16[96,3072]{1,0:T(8,128)(2,1)}, f32[8,128]{1,0:T(8,128)}, /*index=5*/bf16[512,768]{1,0:T(8,128)(2,1)}) custom-call(bf16[512,3072]{1,0:T(8,128)(2,1)} %get-tuple-element.39.refs_0_, bf16[512,3072]{1,0:T(8,128)(2,1)} %get-tuple-element.40.refs_1_, ...), custom_call_target="tpu_custom_call" | custom-call | tf_op jit(solution)/shard_map/sum_grads/pallas_call | solution.py:1224
  222.6 0.0 copy-start.3
  222.6 0.0 copy-start.2
  222.6 1.3 slice_bitcast_fusion
  223.9 1.6 slice_convert_fusion.1
  225.6 2.0 slice_convert_fusion
  227.6 2.2 convert_element_type.29
  229.7 0.0 copy-done.3
  229.7 0.0 copy-start
  229.7 1.1 convert_element_type.30
  230.9 0.0 copy-done.2
  230.9 0.0 copy-start.1
  230.9 0.6 reshape.36
  231.4 1.2 copy.25
  232.7 0.0 copy-done
  232.7 0.9 copy.28
  233.5 0.0 copy-done.1
  233.5 0.9 copy.29
  (1 shorter events, 0.0 us)
Async XLA Ops:
  222.6 7.2 %copy-start.3 = (bf16[96,3072]{1,0:T(8,128)(2,1)S(1)}, bf16[96,3072]{1,0:T(8,128)(2,1)}, u32[]{:S(2)}) copy-start(bf16[96,3072]{1,0:T(8,128)(2,1)} %get-tuple-element.62) | copy-start | bytes 1769476
  222.6 8.3 %copy-start.2 = (bf16[96,3072]{1,0:T(8,128)(2,1)S(1)}, bf16[96,3072]{1,0:T(8,128)(2,1)}, u32[]{:S(2)}) copy-start(bf16[96,3072]{1,0:T(8,128)(2,1)} %get-tuple-element.63) | copy-start | bytes 1769476
  229.7 2.9 %copy-start = (bf16[512,768]{1,0:T(8,128)(2,1)S(1)}, bf16[512,768]{1,0:T(8,128)(2,1)}, u32[]{:S(2)}) copy-start(bf16[512,768]{1,0:T(8,128)(2,1)} %get-tuple-element.80) | copy-start | bytes 2359300
  230.9 2.7 %copy-start.1 = (bf16[512,768]{1,0:T(8,128)(2,1)S(1)}, bf16[512,768]{1,0:T(8,128)(2,1)}, u32[]{:S(2)}) copy-start(bf16[512,768]{1,0:T(8,128)(2,1)} %get-tuple-element.81) | copy-start | bytes 2359300
